TPU v7x, 32 devices: a 4x4x1 block of a 4x4x8 slice. The times are simulated.
32 devices in a mesh: data: 1 (over z), tensor: 32 (over y, x, core).
Axes of the slice: x: 4, y: 4, z: 1, core: 2. Of those that a mesh axis runs over, the one named last changes fastest.
The devices are a block of a 4x4x8 slice.
Arguments:
- token_ids: int32 [8192], P(('data', 'tensor'))
- emb_table: bfloat16 [384, 1472], P('tensor')
- norm_gain: bfloat16 [1472], replicated
- w_up: bfloat16 [1472, 3584], P(None, 'tensor')
- w_down: bfloat16 [3584, 1472], P('tensor')
- grad_out: bfloat16 [8192, 1472], P(('data', 'tensor'))
Outputs:
- output 1: bfloat16 [8192, 1472], P(('data', 'tensor'))
- output 2: float32 [384, 1472], P(('data', 'tensor'))
- output 3: float32 [1472, 3584], P('data', 'tensor')
- output 4: float32 [3584, 1472], P(('data', 'tensor'))
All inputs are finite; a program needn't handle non-finite values.
Results may differ from a plain program's by a relative error of at most 0.00926022.
Values are sent between devices in bfloat16 or wider.
A program may use at most 768 MiB of HBM per device.

v0:
```python
import jax
import jax.numpy as jnp
from jax import lax
from jax.sharding import PartitionSpec as P

EPS = 1e-6


def rms_norm(x_rows, gain_f):
    inv_rms = lax.rsqrt(jnp.mean(x_rows * x_rows, axis=-1, keepdims=True) + EPS)
    return x_rows * inv_rms * gain_f


def gelu_tanh(values):
    return jax.nn.gelu(values, approximate=True)


def contract_last(left_op, right_op):
    return lax.dot_general(left_op, right_op, (((1,), (1,)), ((), ())), preferred_element_type=jnp.float32)


def contract_first(left_op, right_op):
    return lax.dot_general(left_op, right_op, (((0,), (0,)), ((), ())), preferred_element_type=jnp.float32)


def solution(mesh):
    tok_spec = P(('data', 'tensor'))
    row_spec = P(('data', 'tensor'), None)

    def local_step(token_ids, emb_shard, norm_gain, w_up, w_down, grad_out):
        vocab_local = emb_shard.shape[0]
        offset = lax.axis_index('tensor') * vocab_local
        ids_all = lax.all_gather(token_ids, 'tensor', tiled=True)
        rel_ids = ids_all - offset
        is_owned = (rel_ids >= 0) & (rel_ids < vocab_local)
        looked_up = jnp.take(emb_shard, jnp.clip(rel_ids, 0, vocab_local - 1), axis=0)
        emb_part = jnp.where(is_owned[:, None], looked_up, jnp.zeros((), looked_up.dtype))
        x_local = lax.psum_scatter(emb_part, 'tensor', scatter_dimension=0, tiled=True)
        x_f = x_local.astype(jnp.float32)
        gain_f = norm_gain.astype(jnp.float32)
        normed_f, norm_back = jax.vjp(lambda x_in: rms_norm(x_in, gain_f), x_f)
        normed = normed_f.astype(jnp.bfloat16)
        normed_all = lax.all_gather(normed, 'tensor', tiled=True)
        pre_act = jnp.dot(normed_all, w_up, preferred_element_type=jnp.float32).astype(jnp.bfloat16)
        act_f, gelu_back = jax.vjp(gelu_tanh, pre_act.astype(jnp.float32))
        hidden = act_f.astype(jnp.bfloat16)
        y_part = jnp.dot(hidden, w_down, preferred_element_type=jnp.float32)
        y_local = lax.psum_scatter(y_part, 'tensor', scatter_dimension=0, tiled=True)
        out_local = (x_f + y_local).astype(jnp.bfloat16)
        grad_all = lax.all_gather(grad_out, 'tensor', tiled=True)
        d_hidden = contract_last(grad_all, w_down)
        d_pre = gelu_back(d_hidden)[0].astype(jnp.bfloat16)
        d_w_down = contract_first(hidden, grad_all)
        d_w_up = contract_first(normed_all, d_pre)
        d_norm_part = contract_last(d_pre, w_up)
        d_norm = lax.psum_scatter(d_norm_part, 'tensor', scatter_dimension=0, tiled=True)
        dx_local = (grad_out.astype(jnp.float32) + norm_back(d_norm)[0]).astype(jnp.bfloat16)
        dx_all = lax.all_gather(dx_local, 'tensor', tiled=True)
        seg_ids = jnp.where(is_owned, rel_ids, vocab_local)
        d_emb = jax.ops.segment_sum(dx_all.astype(jnp.float32), seg_ids, num_segments=vocab_local + 1)[:vocab_local]
        return out_local, d_emb, d_w_up, d_w_down

    return jax.shard_map(
        local_step,
        mesh=mesh,
        in_specs=(tok_spec, P('tensor', None), P(None), P(None, 'tensor'), P('tensor', None), row_spec),
        out_specs=(row_spec, row_spec, P('data', 'tensor'), row_spec),
        check_vma=False,
    )
```

profile of v0, /device:TPU:97, one launch (start us, length us, event | category | flops | bytes accessed | tf_op | source)
XLA Modules:
  0.0 1110.6 jit_solution(3692451116922677371)
XLA Ops:
  7.2 0.1 reduce-scatter.4.cloned.1.call-start
  7.3 31.8 %all-gather = s32[32,1,256]{2,1,0:T(1,128)S(1)} all-gather(s32[1,1,256]{2,1,0:T(1,128)} %bitcast.19), channel_id=1, replica_groups=mesh['data'=1,'tensor'=32] {'tensor'}, dimensions={0}, use_global_device_ids=true | all-gather | bytes 33792 | tf_op jit(solution)/shard_map/all_gather | solution.py:33
  39.2 0.6 broadcast_select_fusion
  39.8 37.5 %gather_fusion = bf16[8192,1472]{1,0:T(8,128)(2,1)} fusion(bf16[12,1472]{1,0:T(8,128)(2,1)S(1)} %copy-done.2, s32[8192]{0:T(1024)S(1)} %get-tuple-element.7), kind=kCustom, calls=%fused_computation | custom fusion | bytes 48267264 | tf_op jit(solution)/shard_map/jit(_take)/gather | solution.py:36
  77.3 29.7 %copy.13 = bf16[8192,1472]{0,1:T(8,128)(2,1)} copy(bf16[8192,1472]{1,0:T(8,128)(2,1)} %gather_fusion) | data formatting | bytes 48234496 | tf_op jit(solution)/shard_map/jit(_take)/gather | solution.py:36
  107.0 20.5 %select_select_fusion = bf16[8192,1472]{0,1:T(8,128)(2,1)} fusion(bf16[8192,1472]{0,1:T(8,128)(2,1)} %copy.13, pred[8192]{0:T(1024)(128)(4,1)S(1)} %get-tuple-element.9, pred[8192]{0:T(1024)(128)(4,1)S(1)} %get-tuple-element.8), kind=kLoop, calls=%fused_computation.2 | loop fusion | flops 24117248 | bytes 48250880 | tf_op jit(solution)/shard_map/jit(_where)/select_n | solution.py:37
  127.5 0.1 all-gather.7.cloned.1.call-start
  127.6 0.7 all-gather.7.cloned.1.call-update
  128.3 0.1 all-gather.5.cloned.1.call-start
  128.4 131.4 %reduce-scatter.4.cloned.1.call-done = bf16[256,1472]{0,1:T(8,128)(2,1)} async-done(((bf16[8192,1472]{0,1:T(8,128)(2,1)}), bf16[256,1472]{0,1:T(8,128)(2,1)}) %reduce-scatter.4.cloned.1.call-update) | async-done | bytes 753680 | tf_op jit(solution)/shard_map/reduce_scatter | solution.py:38
  259.8 1.3 fusion.10
  261.2 2.3 fusion.12
  263.5 0.2 reduce-scatter.8.cloned.1.call-start
  263.8 91.5 %all-gather.7.cloned.1.call-done = bf16[8192,1472]{0,1:T(8,128)(2,1)} async-done(((bf16[256,1472]{0,1:T(8,128)(2,1)}), bf16[8192,1472]{0,1:T(8,128)(2,1)}) %all-gather.7.cloned.1.call-update) | async-done | bytes 24117264 | tf_op jit(solution)/shard_map/all_gather | solution.py:50
  355.2 13.1 %fusion.23 = f32[8192,112]{0,1:T(8,128)} fusion(bf16[112,1472]{1,0:T(8,128)(2,1)S(1)} %copy-done.4, bf16[8192,1472]{0,1:T(8,128)(2,1)} %all-gather.7.cloned.1.call-done), kind=kOutput, calls=%fused_computation.43 | convolution fusion | flops 2701131776 | bytes 28116992 | tf_op jit(solution)/shard_map/dot_general | solution.py:19
  368.3 83.2 %all-gather.5.cloned.1.call-done = bf16[8192,1472]{0,1:T(8,128)(2,1)} async-done(((bf16[256,1472]{0,1:T(8,128)(2,1)}), bf16[8192,1472]{0,1:T(8,128)(2,1)}) %all-gather.5.cloned.1.call-update) | async-done | bytes 24117264 | tf_op jit(solution)/shard_map/all_gather | solution.py:43
  451.6 13.2 %fusion.7 = (bf16[8192,112]{0,1:T(8,128)(2,1)S(1)}, f32[8192,112]{0,1:T(8,128)}) fusion(f32[8192,112]{0,1:T(8,128)} %fusion.23, bf16[1472,112]{0,1:T(8,128)(2,1)S(1)} %copy-done, bf16[8192,1472]{0,1:T(8,128)(2,1)} %all-gather.5.cloned.1.call-done), kind=kOutput, calls=%fused_computation.13 | convolution fusion | flops 2721316864 | bytes 33622016 | tf_op jit(solution)/shard_map/dot_general | solution.py:44
  464.8 18.6 %fusion.21 = f32[8192,1472]{0,1:T(8,128)} fusion(bf16[8192,112]{0,1:T(8,128)(2,1)S(1)} %get-tuple-element.10, bf16[1472,112]{0,1:T(8,128)(2,1)S(1)} %copy-done), kind=kOutput, calls=%fused_computation.41 | convolution fusion | flops 2701131776 | bytes 50399232 | tf_op jit(solution)/shard_map/dot_general | solution.py:19
  483.4 0.1 reduce-scatter.8.cloned.1.call-update
  483.5 0.3 reduce-scatter.6.cloned.1.call-start
  483.7 20.8 %fusion.20 = f32[8192,1472]{0,1:T(8,128)} fusion(bf16[112,1472]{1,0:T(8,128)(2,1)S(1)} %copy-done.4, f32[8192,112]{0,1:T(8,128)} %get-tuple-element.11), kind=kOutput, calls=%fused_computation.40 | convolution fusion | flops 2709389312 | bytes 52234240 | tf_op jit(solution)/shard_map/dot_general | solution.py:47
  504.6 0.1 all-gather.9.cloned.1.call-start
  504.7 181.6 %reduce-scatter.8.cloned.1.call-done = f32[256,1472]{0,1:T(8,128)} async-done(((f32[8192,1472]{0,1:T(8,128)}), f32[256,1472]{0,1:T(8,128)}) %reduce-scatter.8.cloned.1.call-update) | async-done | bytes 1507344 | tf_op jit(solution)/shard_map/reduce_scatter | solution.py:56
  686.3 1.7 fusion.14
  688.0 204.3 %reduce-scatter.6.cloned.1.call-done = f32[256,1472]{0,1:T(8,128)} async-done(((f32[8192,1472]{0,1:T(8,128)}), f32[256,1472]{0,1:T(8,128)}) %reduce-scatter.6.cloned.1.call-update) | async-done | bytes 1507344 | tf_op jit(solution)/shard_map/reduce_scatter | solution.py:48
  892.2 3.7 fusion.9
  896.0 0.1 all-gather.9.cloned.1.call-update
  896.0 13.0 %fusion.22 = f32[1472,112]{0,1:T(8,128)} fusion(bf16[8192,1472]{0,1:T(8,128)(2,1)} %all-gather.5.cloned.1.call-done, bf16[8192,112]{0,1:T(8,128)(2,1)S(1)} %get-tuple-element.10), kind=kOutput, calls=%fused_computation.42 | convolution fusion | flops 2701131776 | bytes 26611712 | tf_op jit(solution)/shard_map/dot_general | solution.py:23
  909.0 13.7 %fusion.19 = f32[112,1472]{1,0:T(8,128)} fusion(bf16[8192,1472]{0,1:T(8,128)(2,1)} %all-gather.7.cloned.1.call-done, f32[8192,112]{0,1:T(8,128)} %get-tuple-element.11), kind=kOutput, calls=%fused_computation.39 | convolution fusion | flops 2709389312 | bytes 28446720 | tf_op jit(solution)/shard_map/dot_general | solution.py:23
  922.7 66.8 %all-gather.9.cloned.1.call-done = bf16[8192,1472]{0,1:T(8,128)(2,1)} async-done(((bf16[256,1472]{0,1:T(8,128)(2,1)}), bf16[8192,1472]{0,1:T(8,128)(2,1)}) %all-gather.9.cloned.1.call-update) | async-done | bytes 24117264 | tf_op jit(solution)/shard_map/all_gather | solution.py:58
  989.5 33.7 %copy.14 = f32[8192,1472]{1,0:T(8,128)} copy(bf16[8192,1472]{0,1:T(8,128)(2,1)} %all-gather.9.cloned.1.call-done) | data formatting | bytes 72351744 | tf_op jit(solution)/shard_map/convert_element_type | solution.py:60
  1023.2 80.5 %scatter_custom_fusion = f32[13,1472]{1,0:T(8,128)} fusion(s32[8192]{0:T(1024)} %get-tuple-element.6, f32[8192,1472]{1,0:T(8,128)} %copy.14, f32[]{:T(128)} %constant.22.clone.1), kind=kCustom, calls=%fused_computation.29 | custom fusion | flops 12058624 | bytes 77056 | tf_op jit(solution)/shard_map/scatter-add | solution.py:60
  (20 shorter events, 0.3 us)
Async XLA Ops:
  7.2 444.4 %copy-start = (bf16[1472,112]{0,1:T(8,128)(2,1)S(1)}, bf16[1472,112]{0,1:T(8,128)(2,1)}, u32[]{:S(2)}) copy-start(bf16[1472,112]{0,1:T(8,128)(2,1)} %param.9) | copy-start | bytes 989188
  7.2 32.6 %copy-start.2 = (bf16[12,1472]{1,0:T(8,128)(2,1)S(1)}, bf16[12,1472]{1,0:T(8,128)(2,1)}, u32[]{:S(2)}) copy-start(bf16[12,1472]{1,0:T(8,128)(2,1)} %param.7) | copy-start | bytes 105988
  7.2 252.6 %reduce-scatter.4.cloned.1.call-start = ((), (), s32[]{:S(2)}) async-start(), calls=%async_computation.3 | async-start | bytes 24870912 | tf_op jit(solution)/shard_map/reduce_scatter | solution.py:38
  127.4 1.0 copy-start.5
  127.5 227.7 %copy-start.4 = (bf16[112,1472]{1,0:T(8,128)(2,1)S(1)}, bf16[112,1472]{1,0:T(8,128)(2,1)}, u32[]{:S(2)}) copy-start(bf16[112,1472]{1,0:T(8,128)(2,1)} %param.10) | copy-start | bytes 989188
  127.5 227.7 %all-gather.7.cloned.1.call-start = ((), (), s32[]{:S(2)}) async-start(), calls=%async_computation.6 | async-start | bytes 24870912 | tf_op jit(solution)/shard_map/all_gather | solution.py:50
  128.3 323.3 %all-gather.5.cloned.1.call-start = ((), (), s32[]{:S(2)}) async-start(), calls=%async_computation.4 | async-start | bytes 24870912 | tf_op jit(solution)/shard_map/all_gather | solution.py:43
  263.5 422.8 %reduce-scatter.8.cloned.1.call-start = ((), (), s32[]{:S(2)}) async-start(), calls=%async_computation.7 | async-start | bytes 49741824 | tf_op jit(solution)/shard_map/reduce_scatter | solution.py:56
  483.5 408.8 %reduce-scatter.6.cloned.1.call-start = ((), (), s32[]{:S(2)}) async-start(), calls=%async_computation.5 | async-start | bytes 49741824 | tf_op jit(solution)/shard_map/reduce_scatter | solution.py:48
  504.5 181.8 %copy-start.3 = (bf16[256,1472]{0,1:T(8,128)(2,1)S(1)}, bf16[256,1472]{0,1:T(8,128)(2,1)}, u32[]{:S(2)}) copy-start(bf16[256,1472]{0,1:T(8,128)(2,1)} %reduce-scatter.4.cloned.1.call-done) | copy-start | bytes 2260996
  504.6 484.9 %all-gather.9.cloned.1.call-start = ((), (), s32[]{:S(2)}) async-start(), calls=%async_computation.8 | async-start | bytes 24870912 | tf_op jit(solution)/shard_map/all_gather | solution.py:58
  989.5 114.3 %copy-start.1 = (bf16[1472,112]{0,1:T(8,128)(2,1)S(1)}, bf16[1472,112]{0,1:T(8,128)(2,1)}, u32[]{:S(2)}) copy-start(bf16[1472,112]{0,1:T(8,128)(2,1)} %param.9) | copy-start | bytes 989188
Sparse Core Ops, SparseCore 0:
  127.6 132.1 reduce-scatter.3
  261.8 93.3 all-gather.6
  357.8 93.7 all-gather.4
  483.6 202.6 reduce-scatter.7
  690.0 202.1 reduce-scatter.5
  896.2 93.2 all-gather.8
where the time goes:
time: 1110 us
  waiting for transfers between devices  760 us (68%)
  other arithmetic  111 us (10%)
  local copies, waits for them, and re-layouts  101 us (9%)
  matrix products  92.3 us (8%)
  blocking collectives  31.8 us (3%)
  between operations  14.2 us (1%)
    reduce_scatter x1, waiting for transfers between devices, local_step(): lax.psum_scatter(y_part, 'tensor', scatter_dimension=0, tiled=True)  204 us
    reduce_scatter x1, waiting for transfers between devices, local_step(): lax.psum_scatter(d_norm_part, 'tensor', scatter_dimension=0, tiled=True)  182 us
    reduce_scatter x1, waiting for transfers between devices, local_step(): lax.psum_scatter(emb_part, 'tensor', scatter_dimension=0, tiled=True)  131 us
    all_gather x1, waiting for transfers between devices, local_step(): grad_all = lax.all_gather(grad_out, 'tensor', tiled=True)  91.5 us
    all_gather x1, waiting for transfers between devices, local_step(): normed_all = lax.all_gather(normed, 'tensor', tiled=True)  83.2 us
    scatter-add x1, other arithmetic, local_step(): jax.ops.segment_sum(dx_all.astype(jnp.float32), seg_ids, num_segments=voc...  80.5 us
    gather x2, local copies, waits for them, and re-layouts, local_step(): jnp.take(emb_shard, jnp.clip(rel_ids, 0, vocab_local - 1), axis=0)  67.2 us
    all_gather x1, waiting for transfers between devices, local_step(): dx_all = lax.all_gather(dx_local, 'tensor', tiled=True)  66.8 us
  transfers between devices with their start and end apart: 6, of which 6 were waited for; matrix products, arithmetic and copies ran while one was open for 6% of the time, Pallas kernels for 0%

commit v1 on v0

v1 whole, which is shorter than its diff:
```python
import functools
import math

import jax
import jax.numpy as jnp
from jax import lax
from jax.experimental import pallas as pl
from jax.experimental.pallas import tpu as pltpu
from jax.sharding import PartitionSpec as P

EPS = 1e-6
BF = jnp.bfloat16
F32 = jnp.float32
CORES = 2
MESH = pl.DeviceIdType.MESH


def gelu_tanh(values):
    return jax.nn.gelu(values, approximate=True)


def parts(v):
    hi = v.astype(BF)
    r = v - hi.astype(F32)
    mid = r.astype(BF)
    lo = (r - mid.astype(F32)).astype(BF)
    return hi, mid, lo


def dot(a, b, ca, cb):
    return lax.dot_general(a, b, (((ca,), (cb,)), ((), ())), preferred_element_type=F32)


def pack(v):
    half = v.shape[1] // 2
    return jnp.concatenate([v[:, :half], v[:, half:]], axis=0).astype(BF)


class Ring:
    def __init__(self, side):
        me = lax.axis_index('tensor')
        self.side = side
        self.core = core = lax.rem(me, CORES)
        self.chip = chip = me // CORES
        x, y = lax.rem(chip, side), chip // side
        self.a = x * (1 - core) + y * core
        self.b = y * (1 - core) + x * core
        self.partner = {'tensor': me + 1 - 2 * core}

    def at(self, da, db):
        a = lax.rem(self.a + da, self.side)
        b = lax.rem(self.b + db, self.side)
        return a * (1 + (self.side - 1) * self.core) + b * (self.side - (self.side - 1) * self.core)

    def dev(self, da, db):
        return {'tensor': self.at(da, db) * CORES + self.core}


PLUS, MINUS = (2, 1), (3, 0)


class Scatter:
    def __init__(self, ring, g, relay, ra, rb, r, ssem, rsem):
        self.ring, self.g, self.relay, self.ra, self.rb, self.r = ring, g, relay, ra, rb, r
        self.ssem, self.rsem = ssem, rsem
        self.sent = []

    def copy(self, src, dst, i, dev):
        return pltpu.make_async_remote_copy(
            src_ref=src, dst_ref=dst, send_sem=self.ssem.at[i], recv_sem=self.rsem.at[i],
            device_id=dev, device_id_type=MESH)

    def c_relay(self, k):
        da = 1 if k in PLUS else 3
        return self.copy(self.g.at[self.ring.at(2, k)], self.relay.at[k], k, self.ring.dev(da, 0))

    def c_ring(self, k, plus):
        da = 1 if plus else 3
        j = 0 if plus else 1
        return self.copy(self.g.at[self.ring.at(da, k)], self.ra.at[j, k], 4 + 4 * j + k, self.ring.dev(da, 0))

    def c_b(self, k):
        return self.copy(self.r.at[k], self.rb.at[k - 1], 11 + k, self.ring.dev(0, k))

    def go(self, c):
        c.start()
        self.sent.append(c)

    def start(self):
        for kp, km in zip(PLUS, MINUS):
            self.go(self.c_relay(kp))
            self.go(self.c_relay(km))
        for kp, km in zip(MINUS, PLUS):
            self.go(self.c_ring(kp, True))
            self.go(self.c_ring(km, False))

    def middle(self):
        for kp, km in zip(PLUS, MINUS):
            for k, plus in ((kp, True), (km, False)):
                self.c_relay(k).wait_recv()
                blk = self.ring.at(1 if plus else 3, k)
                self.g[blk] = self.g[blk] + self.relay[k]
                self.go(self.c_ring(k, plus))

    def short(self):
        for k in (2, 3, 1, 0):
            self.c_ring(k, True).wait_recv()
            self.c_ring(k, False).wait_recv()
            self.r[k] = self.g[self.ring.at(0, k)] + self.ra[0, k] + self.ra[1, k]
            if k:
                self.go(self.c_b(k))

    def finish(self):
        acc = self.r[0]
        for k in (1, 3, 2):
            self.c_b(k).wait_recv()
            acc = acc + self.rb[k - 1]
        return acc

    def drain(self):
        for c in self.sent:
            c.wait_send()


FWD_P, FWD_M = (0, 2), (3, 1)


class Gather:
    def __init__(self, ring, buf, ssem, rsem, dsem, esem):
        self.ring, self.buf = ring, buf
        self.ssem, self.rsem, self.dsem, self.esem = ssem, rsem, dsem, esem
        self.sent = []

    def copy(self, blk, i, dev):
        ref = self.buf.at[self.ring.core, blk]
        return pltpu.make_async_remote_copy(
            src_ref=ref, dst_ref=ref, send_sem=self.ssem.at[i], recv_sem=self.rsem.at[i],
            device_id=dev, device_id_type=MESH)

    def back(self, k):
        return (self.ring.side - k) % self.ring.side

    def go(self, c):
        c.start()
        self.sent.append(c)

    def over(self, blk):
        ref = self.buf.at[self.ring.core, blk]
        c = pltpu.make_async_remote_copy(
            src_ref=ref, dst_ref=ref, send_sem=self.esem.at[blk], recv_sem=self.dsem.at[blk],
            device_id=self.ring.partner, device_id_type=MESH)
        self.go(c)

    def both(self, k):
        blk = self.ring.at(0, self.back(k))
        self.go(self.copy(blk, k, self.ring.dev(1, 0)))
        self.go(self.copy(blk, 4 + k, self.ring.dev(3, 0)))

    def start(self):
        blk = self.ring.at(0, 0)
        for k in (2, 1, 3):
            self.go(self.copy(blk, 11 + k, self.ring.dev(0, k)))
        self.both(0)
        self.over(blk)

    def first(self):
        for k in (1, 3, 2):
            blk = self.ring.at(0, self.back(k))
            self.copy(blk, 11 + k, self.ring.dev(0, k)).wait_recv()
            self.both(k)
            self.over(blk)

    def middle(self):
        for k in (0, 1, 3, 2):
            blk = self.ring.at(3, self.back(k))
            self.copy(blk, k, self.ring.dev(1, 0)).wait_recv()
            if k in FWD_P:
                self.go(self.copy(blk, 8 + k, self.ring.dev(1, 0)))
            self.over(blk)
            blk = self.ring.at(1, self.back(k))
            self.copy(blk, 4 + k, self.ring.dev(3, 0)).wait_recv()
            if k in FWD_M:
                self.go(self.copy(blk, 8 + k, self.ring.dev(3, 0)))
            self.over(blk)

    def last(self):
        for k in (0, 3, 1, 2):
            blk = self.ring.at(2, self.back(k))
            self.copy(blk, 8 + k, self.ring.dev(1, 0)).wait_recv()
            self.over(blk)

    def finish(self):
        n = self.ring.side * self.ring.side
        for blk in range(n):
            ref = self.buf.at[1 - self.ring.core, blk]
            pltpu.make_async_remote_copy(
                src_ref=ref, dst_ref=ref, send_sem=self.esem.at[blk], recv_sem=self.dsem.at[blk],
                device_id=self.ring.partner, device_id_type=MESH).wait_recv()

    def drain(self):
        for c in self.sent:
            c.wait_send()


def kernel(side, ids_in, e_in, g_in, w1_in, w2_in, d_in, out_ref, de_ref, dw1_ref, dw2_ref, s):
    ring = Ring(side)
    core, chip, partner = ring.core, ring.chip, ring.partner
    chips = side * side
    rows_e, width = e_in.shape
    f_loc = w1_in.shape[0]
    half = s['w1p'].shape[2]
    rest = width - half
    rb = s['gs'].shape[1]
    vocab = chips * rb

    def local(src, dst, i):
        return pltpu.make_async_copy(src, dst, s['lsem'].at[i])

    def pair(src, dst, i):
        return pltpu.make_async_remote_copy(
            src_ref=src, dst_ref=dst, send_sem=s['psem'].at[i], recv_sem=s['qsem'].at[i],
            device_id=partner, device_id_type=MESH)

    c_e = local(e_in, s['es'].at[core], 0)
    c_g = local(g_in, s['gsrc'], 1)
    c_i = local(ids_in, s['ids'].at[core], 2)
    c_w1 = local(w1_in, s['w1s'].at[core], 3)
    c_w2 = local(w2_in, s['w2s'].at[core], 4)
    d_own = (local(d_in.at[:half], s['dt'].at[0], 5),
             local(d_in.at[half:], s['dt'].at[0, :rest], 5))
    r_e = pair(e_in, s['es'].at[core], 0)
    r_i = pair(ids_in, s['ids'].at[core], 1)
    r_w1 = pair(w1_in, s['w1s'].at[core], 2)
    r_w2 = pair(w2_in, s['w2s'].at[core], 3)
    d_give = (pair(d_in.at[half:], s['dt'].at[1, :rest], 4),
              pair(d_in.at[:half], s['dt'].at[1], 4))

    for c in (c_e, c_g, c_i):
        c.start()

    @pl.when(core == 1)
    def _():
        for j in range(2):
            s['dt'][j, rest:, :] = jnp.zeros((half - rest, s['dt'].shape[2]), BF)

    barrier = pltpu.get_barrier_semaphore()
    peers = [partner, ring.dev(1, 0), ring.dev(3, 0)] + [ring.dev(0, k) for k in (1, 2, 3)]
    for p in peers:
        pl.semaphore_signal(barrier, inc=1, device_id=p, device_id_type=MESH)
    for i in range(2):
        @pl.when(core == i)
        def _():
            d_own[i].start()
    c_w1.start()
    c_w2.start()
    pl.semaphore_wait(barrier, len(peers))

    r_e.start()
    r_i.start()
    for i in range(2):
        @pl.when(core == i)
        def _():
            d_give[i].start()
    r_w1.start()
    r_w2.start()

    def wide(v):
        return jnp.concatenate([v, jnp.zeros((v.shape[0], 2 * half - width), F32)], axis=1)

    c_e.wait()
    c_g.wait()
    r_e.wait_recv()
    gain = wide(s['gsrc'][...].astype(F32))
    for i in range(2):
        s['e24'][i * rows_e:(i + 1) * rows_e, :] = wide(s['es'][i].astype(F32))

    def inv_rms(x):
        return lax.rsqrt(jnp.sum(x * x, axis=-1, keepdims=True) / width + EPS)

    def mine(v):
        return jnp.where(core == 0, v[:, :half], v[:, half:])

    x24 = s['e24'][...]
    ag_n = Gather(ring, s['bn'], s['nss'], s['nrs'], s['nds'], s['nes'])
    s['bn'][core, chip] = pack(mine(x24 * inv_rms(x24) * gain))
    ag_n.start()

    c_i.wait()
    r_i.wait_recv()
    for i in range(2):
        @pl.when(core == i)
        def _():
            d_own[i].wait()
            d_give[1 - i].wait_recv()

    def hot(ids_row):
        row = lax.broadcasted_iota(jnp.int32, (vocab, ids_row.shape[1]), 0)
        return jnp.where(row == ids_row, 1.0, 0.0).astype(BF)

    tot = dot(hot(s['ids'][core]), s['dt'][0], 1, 1) + dot(hot(s['ids'][1 - core]), s['dt'][1], 1, 1)
    s['gs'][...] = tot.reshape(chips, rb, half)
    rs_s = Scatter(ring, s['gs'], s['lay'].at[0], s['ra'].at[0], s['rb'].at[0], s['r'].at[0], s['ss'].at[0], s['sr'].at[0])
    rs_s.start()

    ag_n.first()

    c_w1.wait()
    c_w2.wait()
    r_w1.wait_recv()
    r_w2.wait_recv()
    for w_src, w_dst in (('w1s', 'w1p'), ('w2s', 'w2p')):
        for i in range(2):
            rows = slice(i * f_loc, (i + 1) * f_loc)
            s[w_dst][0, rows, :] = s[w_src][i, :, :half]
            s[w_dst][1, rows, :] = jnp.concatenate(
                [s[w_src][i, :, half:], jnp.zeros((f_loc, half - rest), BF)], axis=1)

    rs_s.middle()
    ag_n.middle()
    rs_s.short()
    ag_n.last()
    ag_n.finish()

    def unpack(buf, dst):
        q = half // 2
        for h in range(2):
            v = buf[h].astype(F32)
            dst[h, :, :q] = v[:, :rb].reshape(vocab, q).astype(BF)
            dst[h, :, q:] = v[:, rb:].reshape(vocab, q).astype(BF)

    unpack(s['bn'], s['n'])
    pre = (dot(s['n'][0], s['w1p'][0], 1, 1) + dot(s['n'][1], s['w1p'][1], 1, 1)).astype(BF)
    pre_f = pre.astype(F32)
    act, gelu_back = jax.vjp(gelu_tanh, pre_f)
    hid = act.astype(BF)
    s['hid'][...] = hid
    s['slope'][...] = gelu_back(jnp.ones_like(pre_f))[0]
    s['gy'][...] = dot(hid, s['w2p'][core], 1, 0).reshape(chips, rb, half)

    ag_s = Gather(ring, s['bs'], s['sss'], s['srs'], s['sds'], s['ses'])
    s['bs'][core, chip] = rs_s.finish()
    ag_s.start()
    rs_y = Scatter(ring, s['gy'], s['lay'].at[1], s['ra'].at[1], s['rb'].at[1], s['r'].at[1], s['ss'].at[1], s['sr'].at[1])
    rs_y.start()
    ag_s.first()
    ag_s.middle()
    rs_y.middle()
    ag_s.last()
    rs_y.short()
    ag_s.finish()

    def split(i, c):
        v = s['bs'][i].reshape(vocab, half)
        for j, p in enumerate(parts(v)):
            s['sp'][3 * i + j] = p
        return c

    for i in range(2):
        split(i, 0)
    dh = jnp.zeros(s['slope'].shape, F32)
    for j in (2, 1, 0):
        for i in range(2):
            dh = dh + dot(s['sp'][3 * i + j], s['w2p'][i], 1, 1)
    du = dh * s['slope'][...]
    du_p = parts(du)
    dn = jnp.zeros((vocab, half), F32)
    for p in du_p[::-1]:
        dn = dn + dot(p, s['w1p'][core], 1, 0)
    s['gd'][...] = dn.reshape(chips, rb, half)
    rs_d = Scatter(ring, s['gd'], s['lay'].at[2], s['ra'].at[2], s['rb'].at[2], s['r'].at[2], s['ss'].at[2], s['sr'].at[2])
    rs_d.start()

    ag_o = Gather(ring, s['bo'], s['oss'], s['ors'], s['ods'], s['oes'])
    s['bo'][core, chip] = pack(mine(s['e24'][...]) + rs_y.finish())
    ag_o.start()
    rs_d.middle()
    ag_o.first()

    def own(v):
        return jnp.where(core == 0, v[:, :f_loc], v[:, f_loc:])

    hid_own = own(s['hid'][...].astype(F32)).astype(BF)
    for i in range(2):
        acc = jnp.zeros((f_loc, half), F32)
        for j in (2, 1, 0):
            acc = acc + dot(hid_own, s['sp'][3 * i + j], 0, 0)
        if i == 0:
            s['dw2'][:, :half] = acc
        else:
            s['dw2'][:, half:] = acc[:, :rest]
    o_w2 = local(s['dw2'], dw2_ref, 6)
    o_w2.start()

    rs_d.short()
    ag_o.middle()
    du_own = parts(own(du))
    for i in range(2):
        acc = jnp.zeros((f_loc, half), F32)
        for p in du_own[::-1]:
            acc = acc + dot(p, s['n'][i], 0, 0)
        if i == 0:
            s['dw1'][:, :half] = acc
        else:
            s['dw1'][:, half:] = acc[:, :rest]
    o_w1 = local(s['dw1'], dw1_ref, 7)
    o_w1.start()

    s['dnx'][core] = rs_d.finish()
    r_dn = pair(s['dnx'].at[core], s['dnx'].at[core], 5)
    r_dn.start()
    ag_o.last()
    pair(s['dnx'].at[1 - core], s['dnx'].at[1 - core], 5).wait_recv()
    inv = inv_rms(s['e24'][...])
    xr = s['e24'][...] * inv
    gd = gain * jnp.concatenate([s['dnx'][0], s['dnx'][1]], axis=1)
    dx = inv * (gd - xr * (jnp.sum(xr * gd, axis=-1, keepdims=True) / width))
    dx = dx + jnp.concatenate([s['bs'][0, chip], s['bs'][1, chip]], axis=1)
    s['de'][...] = jnp.where(core == 0, dx[:rows_e], dx[rows_e:])[:, :width]
    o_de = local(s['de'], de_ref, 8)
    o_de.start()

    ag_o.finish()
    unpack(s['bo'], s['o'])
    mask = hot(s['ids'][core])
    s['out'][:half] = dot(s['o'][0], mask, 0, 0).astype(BF)
    s['out'][half:] = dot(s['o'][1], mask, 0, 0)[:rest].astype(BF)
    o_out = local(s['out'], out_ref, 9)
    o_out.start()

    for c in (r_e, r_i, r_w1, r_w2, r_dn):
        c.wait_send()
    for i in range(2):
        @pl.when(core == i)
        def _():
            d_give[i].wait_send()
    for x in (ag_n, rs_s, ag_s, rs_y, rs_d, ag_o):
        x.drain()
    for c in (o_w2, o_w1, o_de, o_out):
        c.wait()


def solution(mesh):
    tok_spec = P(('data', 'tensor'))
    row_spec = P(('data', 'tensor'), None)
    n_tensor = mesh.shape['tensor']
    chips = n_tensor // CORES
    side = math.isqrt(chips)
    assert side == 4 and side * side == chips

    def local_step(token_ids, emb_shard, norm_gain, w_up, w_down, grad_out):
        rows_e, width = emb_shard.shape
        tokens = token_ids.shape[0]
        f_loc = w_up.shape[1]
        f_chip = CORES * f_loc
        half = -(-width // 256) * 128
        rb = CORES * rows_e
        vocab = chips * rb
        vm = pltpu.VMEM
        dma = lambda *shape: pltpu.SemaphoreType.DMA(shape)
        scratch = dict(
            es=vm((2, rows_e, width), BF), gsrc=vm((1, width), BF), ids=vm((2, 1, tokens), jnp.int32),
            w1s=vm((2, f_loc, width), BF), w2s=vm((2, f_loc, width), BF), dt=vm((2, half, tokens), BF),
            e24=vm((rb, 2 * half), F32), w1p=vm((2, f_chip, half), BF), w2p=vm((2, f_chip, half), BF),
            bn=vm((2, chips, 2 * rb, half // 2), BF), bo=vm((2, chips, 2 * rb, half // 2), BF),
            bs=vm((2, chips, rb, half), F32), sp=vm((6, vocab, half), BF),
            n=vm((2, vocab, half), BF), o=vm((2, vocab, half), BF),
            gs=vm((chips, rb, half), F32), gy=vm((chips, rb, half), F32), gd=vm((chips, rb, half), F32),
            lay=vm((3, 4, rb, half), F32), ra=vm((3, 2, 4, rb, half), F32), rb=vm((3, 3, rb, half), F32),
            r=vm((3, 4, rb, half), F32),
            hid=vm((vocab, f_chip), BF), slope=vm((vocab, f_chip), F32),
            dnx=vm((2, rb, half), F32), de=vm((rows_e, width), F32),
            dw1=vm((f_loc, width), F32), dw2=vm((f_loc, width), F32), out=vm((width, tokens), BF),
            lsem=dma(10), psem=dma(6), qsem=dma(6),
            ss=dma(3, 15), sr=dma(3, 15),
        )
        for name in 'nso':
            scratch.update({name + 'ss': dma(15), name + 'rs': dma(15), name + 'ds': dma(chips), name + 'es': dma(chips)})
        names = list(scratch)

        def body(*refs):
            kernel(side, *refs[:10], dict(zip(names, refs[10:])))

        hbm = pl.BlockSpec(memory_space=pl.ANY)
        out_t, d_emb, dw1_t, d_w2 = pl.pallas_call(
            body,
            out_shape=(
                jax.ShapeDtypeStruct((width, tokens), BF),
                jax.ShapeDtypeStruct((rows_e, width), F32),
                jax.ShapeDtypeStruct((f_loc, width), F32),
                jax.ShapeDtypeStruct((f_loc, width), F32),
            ),
            in_specs=[hbm] * 6,
            out_specs=(hbm,) * 4,
            scratch_shapes=list(scratch.values()),
            compiler_params=pltpu.CompilerParams(
                collective_id=0, has_side_effects=True, vmem_limit_bytes=60 * 1024 * 1024),
            name='step',
        )(token_ids.reshape(1, tokens), emb_shard, norm_gain.reshape(1, width), w_up.T, w_down, grad_out.T)
        return out_t.T, d_emb, dw1_t.T, d_w2

    return jax.shard_map(
        local_step,
        mesh=mesh,
        in_specs=(tok_spec, P('tensor', None), P(None), P(None, 'tensor'), P('tensor', None), row_spec),
        out_specs=(row_spec, row_spec, P('data', 'tensor'), row_spec),
        check_vma=False,
    )
```

time: 1110 us -> 66.7 us (0.06)
  waiting for transfers between devices: 760 us -> 0 us
  other arithmetic: 111 us -> 0 us
  local copies, waits for them, and re-layouts: 101 us -> 6.23 us
  matrix products: 92.3 us -> 0 us
  Pallas kernels: 0 us -> 59.6 us
  blocking collectives: 31.8 us -> 0 us
  between operations: 14.2 us -> 0.67 us
    reduce_scatter x3 -> x0, waiting for transfers between devices: 517 us -> none  [the longest x1 204 us: local_step(): lax.psum_scatter(y_part, 'tensor', scatter_dimension=0, tiled=True)]
    all_gather x3 -> x0, waiting for transfers between devices: 241 us -> none  [the longest x1 91.5 us: local_step(): grad_all = lax.all_gather(grad_out, 'tensor', tiled=True)]
    dot_general x6 -> x0, matrix products: 92.3 us -> none  [the longest x2 31.7 us: contract_last(): lax.dot_general(left_op, right_op, (((1,), (1,)), ((), ())), preferred_el...]
    scatter-add x1 -> x0, other arithmetic: 80.5 us -> none  [local_step(): jax.ops.segment_sum(dx_all.astype(jnp.float32), seg_ids, num_segments=voc...]
    gather x2 -> x0, local copies, waits for them, and re-layouts: 67.2 us -> none  [local_step(): jnp.take(emb_shard, jnp.clip(rel_ids, 0, vocab_local - 1), axis=0)]
    pallas_call x0 -> x1, Pallas kernels: none -> 59.6 us  [local_step(): pl.pallas_call(body, out_shape=(jax.ShapeDtypeStruct((width, tokens), BF)...]
    convert_element_type x1 -> x0, local copies, waits for them, and re-layouts: 33.7 us -> none  [local_step(): dx_all.astype(jnp.float32)]
    all_gather x1 -> x0, blocking collectives: 31.8 us -> none  [local_step(): ids_all = lax.all_gather(token_ids, 'tensor', tiled=True)]
  transfers between devices with their start and end apart: 6 -> 0, of which waited for: 6 -> 0; matrix products, arithmetic and copies ran while one was open for 6% -> 0% of each run, Pallas kernels for 0% -> 0%
where the time goes in v1:
time: 66.7 us; the launch traced here: 66.5 us
  Pallas kernels  59.6 us (89%)
  local copies, waits for them, and re-layouts  6.23 us (9%)
  between operations  0.67 us (1%)
    pallas_call x1, Pallas kernels, local_step(): pl.pallas_call(body, out_shape=(jax.ShapeDtypeStruct((width, tokens), BF)...  59.6 us
    unnamed x12, local copies, waits for them, and re-layouts  5.63 us

profile of v1, /device:TPU:97, one launch (start us, length us, event | category | flops | bytes accessed | tf_op | source)
XLA Modules:
  0.0 66.5 jit_solution(13237675879711534507)
XLA Ops:
  0.6 0.0 copy-start.3
  0.6 0.7 %copy-done.3 = bf16[1472]{0:T(1024)(128)(2,1)S(1)} copy-done((bf16[1472]{0:T(1024)(128)(2,1)S(1)}, bf16[1472]{0:T(1024)(128)(2,1)}, u32[]{:S(2)}) %copy-start.3) | copy-done | bytes 2968
  1.3 0.6 reshape.15.refs_2_
  1.9 59.6 %step.1 = (bf16[1472,256]{1,0:T(8,128)(2,1)}, f32[12,1472]{1,0:T(8,128)}, f32[112,1472]{1,0:T(8,128)}, f32[112,1472]{1,0:T(8,128)}) custom-call(s32[1,256]{1,0:T(1,128)} %bitcast.9, bf16[12,1472]{1,0:T(8,128)(2,1)} %refs_1_.1, bf16[1,1472]{1,0:T(2,128)(2,1)} %reshape.15.refs_2_, bf16[112,1472]{1,0:T(8,128)(2,1)} %bitcast.8, bf16[112,1472]{1,0:T(8,128)(2,1)} %refs_4_.1, ...), custom_call_target="tpu_custom_call" | custom-call | tf_op jit(solution)/shard_map/step/pallas_call | solution.py:484
  61.5 0.0 copy-start.2
  61.5 0.0 copy-start.1
  61.5 2.1 %copy.14 = bf16[256,1472]{0,1:T(8,128)(2,1)} copy(bf16[256,1472]{0,1:T(8,128)(2,1)} %bitcast.6) | data formatting | bytes 1507328
  63.7 0.0 copy-done.2
  63.7 0.6 copy.15
  64.3 0.0 copy-done.1
  64.3 0.0 copy-start
  64.3 0.8 %copy.16 = f32[1472,112]{0,1:T(8,128)} copy(f32[1472,112]{0,1:T(8,128)S(1)} %bitcast.7) | data formatting | bytes 1318912
  65.2 0.5 copy-done
  65.7 0.8 %copy.17 = f32[112,1472]{1,0:T(8,128)} copy(f32[112,1472]{1,0:T(8,128)S(1)} %copy-done) | data formatting | bytes 1318912
Async XLA Ops:
  0.6 0.7 %copy-start.3 = (bf16[1472]{0:T(1024)(128)(2,1)S(1)}, bf16[1472]{0:T(1024)(128)(2,1)}, u32[]{:S(2)}) copy-start(bf16[1472]{0:T(1024)(128)(2,1)} %param.8) | copy-start | bytes 8836
  61.5 2.1 %copy-start.2 = (f32[12,1472]{1,0:T(8,128)S(1)}, f32[12,1472]{1,0:T(8,128)}, u32[]{:S(2)}) copy-start(f32[12,1472]{1,0:T(8,128)} %get-tuple-element.17) | copy-start | bytes 211972
  61.5 2.8 %copy-start.1 = (f32[112,1472]{1,0:T(8,128)S(1)}, f32[112,1472]{1,0:T(8,128)}, u32[]{:S(2)}) copy-start(f32[112,1472]{1,0:T(8,128)} %get-tuple-element.10) | copy-start | bytes 1978372
  64.3 1.3 %copy-start = (f32[112,1472]{1,0:T(8,128)S(1)}, f32[112,1472]{1,0:T(8,128)}, u32[]{:S(2)}) copy-start(f32[112,1472]{1,0:T(8,128)} %get-tuple-element.19) | copy-start | bytes 1978372

commit v2 on v1

--- a/solution.py
+++ b/solution.py
@@ -34,6 +34,11 @@
 def pack(v):
     half = v.shape[1] // 2
     return jnp.concatenate([v[:, :half], v[:, half:]], axis=0).astype(BF)
+
+
+def hot(ids_row, vocab):
+    row = lax.broadcasted_iota(jnp.int32, (vocab, ids_row.shape[1]), 0)
+    return jnp.where(row == ids_row, 1.0, 0.0).astype(BF)
 
 
 class Ring:
@@ -67,7 +72,7 @@
 
     def copy(self, src, dst, i, dev):
         return pltpu.make_async_remote_copy(
-            src_ref=src, dst_ref=dst, send_sem=self.ssem.at[i], recv_sem=self.rsem.at[i],
+            src_ref=src, dst_ref=dst, send_sem=self.ssem, recv_sem=self.rsem.at[i],
             device_id=dev, device_id_type=MESH)
 
     def c_relay(self, k):
@@ -86,10 +91,12 @@
         c.start()
         self.sent.append(c)
 
-    def start(self):
+    def start_relay(self):
         for kp, km in zip(PLUS, MINUS):
             self.go(self.c_relay(kp))
             self.go(self.c_relay(km))
+
+    def start_own(self):
         for kp, km in zip(MINUS, PLUS):
             self.go(self.c_ring(kp, True))
             self.go(self.c_ring(km, False))
@@ -118,8 +125,8 @@
         return acc
 
     def drain(self):
-        for c in self.sent:
-            c.wait_send()
+        whole = self.g.at[pl.ds(0, len(self.sent))]
+        pltpu.make_async_copy(whole, whole, self.ssem).wait()
 
 
 FWD_P, FWD_M = (0, 2), (3, 1)
@@ -134,7 +141,7 @@
     def copy(self, blk, i, dev):
         ref = self.buf.at[self.ring.core, blk]
         return pltpu.make_async_remote_copy(
-            src_ref=ref, dst_ref=ref, send_sem=self.ssem.at[i], recv_sem=self.rsem.at[i],
+            src_ref=ref, dst_ref=ref, send_sem=self.ssem, recv_sem=self.rsem.at[i],
             device_id=dev, device_id_type=MESH)
 
     def back(self, k):
@@ -144,12 +151,11 @@
         c.start()
         self.sent.append(c)
 
-    def over(self, blk):
+    def over(self, blk, stage):
         ref = self.buf.at[self.ring.core, blk]
-        c = pltpu.make_async_remote_copy(
-            src_ref=ref, dst_ref=ref, send_sem=self.esem.at[blk], recv_sem=self.dsem.at[blk],
-            device_id=self.ring.partner, device_id_type=MESH)
-        self.go(c)
+        pltpu.make_async_remote_copy(
+            src_ref=ref, dst_ref=ref, send_sem=self.esem, recv_sem=self.dsem.at[stage],
+            device_id=self.ring.partner, device_id_type=MESH).start()
 
     def both(self, k):
         blk = self.ring.at(0, self.back(k))
@@ -161,53 +167,56 @@
         for k in (2, 1, 3):
             self.go(self.copy(blk, 11 + k, self.ring.dev(0, k)))
         self.both(0)
-        self.over(blk)
+        self.over(blk, 0)
 
     def first(self):
         for k in (1, 3, 2):
             blk = self.ring.at(0, self.back(k))
             self.copy(blk, 11 + k, self.ring.dev(0, k)).wait_recv()
             self.both(k)
-            self.over(blk)
-
-    def middle(self):
-        for k in (0, 1, 3, 2):
+            self.over(blk, 0)
+
+    def middle(self, ks=(0, 1, 3, 2)):
+        for k in ks:
             blk = self.ring.at(3, self.back(k))
             self.copy(blk, k, self.ring.dev(1, 0)).wait_recv()
             if k in FWD_P:
                 self.go(self.copy(blk, 8 + k, self.ring.dev(1, 0)))
-            self.over(blk)
+            self.over(blk, 1)
             blk = self.ring.at(1, self.back(k))
             self.copy(blk, 4 + k, self.ring.dev(3, 0)).wait_recv()
             if k in FWD_M:
                 self.go(self.copy(blk, 8 + k, self.ring.dev(3, 0)))
-            self.over(blk)
+            self.over(blk, 1)
 
     def last(self):
         for k in (0, 3, 1, 2):
             blk = self.ring.at(2, self.back(k))
             self.copy(blk, 8 + k, self.ring.dev(1, 0)).wait_recv()
-            self.over(blk)
+            self.over(blk, 2)
+
+    def passed(self, stage):
+        ref = self.buf.at[1 - self.ring.core, pl.ds(0, (4, 8, 4)[stage])]
+        pltpu.make_async_copy(ref, ref, self.dsem.at[stage]).wait()
 
     def finish(self):
-        n = self.ring.side * self.ring.side
-        for blk in range(n):
-            ref = self.buf.at[1 - self.ring.core, blk]
-            pltpu.make_async_remote_copy(
-                src_ref=ref, dst_ref=ref, send_sem=self.esem.at[blk], recv_sem=self.dsem.at[blk],
-                device_id=self.ring.partner, device_id_type=MESH).wait_recv()
+        for stage in range(3):
+            self.passed(stage)
 
     def drain(self):
-        for c in self.sent:
-            c.wait_send()
-
-
-def kernel(side, ids_in, e_in, g_in, w1_in, w2_in, d_in, out_ref, de_ref, dw1_ref, dw2_ref, s):
+        ref = self.buf.at[self.ring.core]
+        pltpu.make_async_copy(ref, ref, self.esem).wait()
+        ref = self.buf.at[0, pl.ds(0, len(self.sent))]
+        pltpu.make_async_copy(ref, ref, self.ssem).wait()
+
+
+def kernel(side, ids_in, e_in, g_in, w1_in, w2_in, d_in, o_ref, de_ref, dw1_ref, dw2_ref, s):
     ring = Ring(side)
     core, chip, partner = ring.core, ring.chip, ring.partner
     chips = side * side
     rows_e, width = e_in.shape
     f_loc = w1_in.shape[0]
+    f_chip = CORES * f_loc
     half = s['w1p'].shape[2]
     rest = width - half
     rb = s['gs'].shape[1]
@@ -270,7 +279,7 @@
     c_e.wait()
     c_g.wait()
     r_e.wait_recv()
-    gain = wide(s['gsrc'][...].astype(F32))
+    gain = wide(s['gsrc'][...].astype(F32).reshape(1, width))
     for i in range(2):
         s['e24'][i * rows_e:(i + 1) * rows_e, :] = wide(s['es'][i].astype(F32))
 
@@ -281,26 +290,27 @@
         return jnp.where(core == 0, v[:, :half], v[:, half:])
 
     x24 = s['e24'][...]
-    ag_n = Gather(ring, s['bn'], s['nss'], s['nrs'], s['nds'], s['nes'])
+    ag_n = Gather(ring, s['bn'], s['gsem'].at[3], s['gr'].at[0], s['gd3'].at[0], s['gsem'].at[6])
     s['bn'][core, chip] = pack(mine(x24 * inv_rms(x24) * gain))
     ag_n.start()
 
     c_i.wait()
-    r_i.wait_recv()
     for i in range(2):
         @pl.when(core == i)
         def _():
             d_own[i].wait()
+    tot = dot(hot(s['ids'][core], vocab), s['dt'][0], 1, 1)
+    r_i.wait_recv()
+    for i in range(2):
+        @pl.when(core == i)
+        def _():
             d_give[1 - i].wait_recv()
 
-    def hot(ids_row):
-        row = lax.broadcasted_iota(jnp.int32, (vocab, ids_row.shape[1]), 0)
-        return jnp.where(row == ids_row, 1.0, 0.0).astype(BF)
-
-    tot = dot(hot(s['ids'][core]), s['dt'][0], 1, 1) + dot(hot(s['ids'][1 - core]), s['dt'][1], 1, 1)
+    tot = tot + dot(hot(s['ids'][1 - core], vocab), s['dt'][1], 1, 1)
     s['gs'][...] = tot.reshape(chips, rb, half)
-    rs_s = Scatter(ring, s['gs'], s['lay'].at[0], s['ra'].at[0], s['rb'].at[0], s['r'].at[0], s['ss'].at[0], s['sr'].at[0])
-    rs_s.start()
+    rs_s = Scatter(ring, s['gs'], s['lay'].at[0], s['ra'].at[0], s['rb'].at[0], s['r'].at[0], s['gsem'].at[0], s['sr'].at[0])
+    rs_s.start_relay()
+    rs_s.start_own()
 
     ag_n.first()
 
@@ -334,47 +344,74 @@
     act, gelu_back = jax.vjp(gelu_tanh, pre_f)
     hid = act.astype(BF)
     s['hid'][...] = hid
-    s['slope'][...] = gelu_back(jnp.ones_like(pre_f))[0]
+    s['slope'][...] = gelu_back(jnp.ones_like(pre_f))[0].reshape(chips, rb, f_chip)
+    s['dh'][...] = jnp.zeros((chips, rb, f_chip), F32)
     s['gy'][...] = dot(hid, s['w2p'][core], 1, 0).reshape(chips, rb, half)
 
-    ag_s = Gather(ring, s['bs'], s['sss'], s['srs'], s['sds'], s['ses'])
+    rs_y = Scatter(ring, s['gy'], s['lay'].at[1], s['ra'].at[1], s['rb'].at[1], s['r'].at[1], s['gsem'].at[1], s['sr'].at[1])
+    ag_s = Gather(ring, s['bs'], s['gsem'].at[4], s['gr'].at[1], s['gd3'].at[1], s['gsem'].at[7])
     s['bs'][core, chip] = rs_s.finish()
     ag_s.start()
-    rs_y = Scatter(ring, s['gy'], s['lay'].at[1], s['ra'].at[1], s['rb'].at[1], s['r'].at[1], s['ss'].at[1], s['sr'].at[1])
-    rs_y.start()
+    rs_y = Scatter(ring, s['gy'], s['lay'].at[1], s['ra'].at[1], s['rb'].at[1], s['r'].at[1], s['gsem'].at[1], s['sr'].at[1])
+    rs_y.start_relay()
+    rs_y.start_own()
     ag_s.first()
-    ag_s.middle()
+
+    def tall(v):
+        return jnp.concatenate(parts(v), axis=0)
+
+    def short(v):
+        n = v.shape[0] // 3
+        return v[2 * n:] + v[n:2 * n] + v[:n]
+
+    def dh_add(h, blks):
+        v = jnp.concatenate([s['bs'][h, blk] for blk in blks], axis=0)
+        d = short(dot(tall(v), s['w2p'][h], 1, 1))
+        for i, blk in enumerate(blks):
+            s['dh'][blk] = s['dh'][blk] + d[i * rb:(i + 1) * rb]
+
+    def line(da):
+        return [ring.at(da, k) for k in range(side)]
+
+    def cross(db):
+        return [ring.at(k, db) for k in range(side)]
+
+    def dn_rows(da):
+        blks = line(da)
+        du = [s['dh'][blk] * s['slope'][blk] for blk in blks]
+        for blk, v in zip(blks, du):
+            s['dh'][blk] = v
+        d = short(dot(tall(jnp.concatenate(du, axis=0)), s['w1p'][core], 1, 0))
+        for i, blk in enumerate(blks):
+            s['gd'][blk] = d[i * rb:(i + 1) * rb]
+
+    ag_s.middle((0,))
+    dh_add(core, line(0))
     rs_y.middle()
+    ag_s.middle((1, 3, 2))
+    dh_add(core, line(1) + line(3))
+    ag_s.passed(0)
+    dh_add(1 - core, cross(0))
+    rs_y.short()
+    ag_s.passed(1)
+    dh_add(1 - core, cross(1) + cross(3))
     ag_s.last()
-    rs_y.short()
-    ag_s.finish()
-
-    def split(i, c):
-        v = s['bs'][i].reshape(vocab, half)
-        for j, p in enumerate(parts(v)):
-            s['sp'][3 * i + j] = p
-        return c
-
-    for i in range(2):
-        split(i, 0)
-    dh = jnp.zeros(s['slope'].shape, F32)
-    for j in (2, 1, 0):
-        for i in range(2):
-            dh = dh + dot(s['sp'][3 * i + j], s['w2p'][i], 1, 1)
-    du = dh * s['slope'][...]
-    du_p = parts(du)
-    dn = jnp.zeros((vocab, half), F32)
-    for p in du_p[::-1]:
-        dn = dn + dot(p, s['w1p'][core], 1, 0)
-    s['gd'][...] = dn.reshape(chips, rb, half)
-    rs_d = Scatter(ring, s['gd'], s['lay'].at[2], s['ra'].at[2], s['rb'].at[2], s['r'].at[2], s['ss'].at[2], s['sr'].at[2])
-    rs_d.start()
-
-    ag_o = Gather(ring, s['bo'], s['oss'], s['ors'], s['ods'], s['oes'])
+    dh_add(core, line(2))
+    ag_s.passed(2)
+    dh_add(1 - core, cross(2))
+    rs_d = Scatter(ring, s['gd'], s['lay'].at[2], s['ra'].at[2], s['rb'].at[2], s['r'].at[2], s['gsem'].at[2], s['sr'].at[2])
+    dn_rows(2)
+    rs_d.start_relay()
+    dn_rows(1)
+    dn_rows(3)
+    rs_d.start_own()
+    dn_rows(0)
+    ag_o = Gather(ring, s['bo'], s['gsem'].at[5], s['gr'].at[2], s['gd3'].at[2], s['gsem'].at[8])
     s['bo'][core, chip] = pack(mine(s['e24'][...]) + rs_y.finish())
     ag_o.start()
-    rs_d.middle()
-    ag_o.first()
+    for i in range(2):
+        for j, p in enumerate(parts(s['bs'][i].reshape(vocab, half))):
+            s['sp'][3 * i + j] = p
 
     def own(v):
         return jnp.where(core == 0, v[:, :f_loc], v[:, f_loc:])
@@ -385,26 +422,25 @@
         for j in (2, 1, 0):
             acc = acc + dot(hid_own, s['sp'][3 * i + j], 0, 0)
         if i == 0:
-            s['dw2'][:, :half] = acc
+            dw2_ref[:, :half] = acc
         else:
-            s['dw2'][:, half:] = acc[:, :rest]
-    o_w2 = local(s['dw2'], dw2_ref, 6)
-    o_w2.start()
-
-    rs_d.short()
-    ag_o.middle()
-    du_own = parts(own(du))
+            dw2_ref[:, half:] = acc[:, :rest]
+
+    rs_d.middle()
+    ag_o.first()
+
+    du_own = parts(own(s['dh'][...].reshape(vocab, f_chip)))
     for i in range(2):
         acc = jnp.zeros((f_loc, half), F32)
         for p in du_own[::-1]:
             acc = acc + dot(p, s['n'][i], 0, 0)
         if i == 0:
-            s['dw1'][:, :half] = acc
+            dw1_ref[:, :half] = acc
         else:
-            s['dw1'][:, half:] = acc[:, :rest]
-    o_w1 = local(s['dw1'], dw1_ref, 7)
-    o_w1.start()
-
+            dw1_ref[:, half:] = acc[:, :rest]
+
+    rs_d.short()
+    ag_o.middle()
     s['dnx'][core] = rs_d.finish()
     r_dn = pair(s['dnx'].at[core], s['dnx'].at[core], 5)
     r_dn.start()
@@ -415,17 +451,10 @@
     gd = gain * jnp.concatenate([s['dnx'][0], s['dnx'][1]], axis=1)
     dx = inv * (gd - xr * (jnp.sum(xr * gd, axis=-1, keepdims=True) / width))
     dx = dx + jnp.concatenate([s['bs'][0, chip], s['bs'][1, chip]], axis=1)
-    s['de'][...] = jnp.where(core == 0, dx[:rows_e], dx[rows_e:])[:, :width]
-    o_de = local(s['de'], de_ref, 8)
-    o_de.start()
+    de_ref[...] = jnp.where(core == 0, dx[:rows_e], dx[rows_e:])[:, :width]
 
     ag_o.finish()
-    unpack(s['bo'], s['o'])
-    mask = hot(s['ids'][core])
-    s['out'][:half] = dot(s['o'][0], mask, 0, 0).astype(BF)
-    s['out'][half:] = dot(s['o'][1], mask, 0, 0)[:rest].astype(BF)
-    o_out = local(s['out'], out_ref, 9)
-    o_out.start()
+    unpack(s['bo'], o_ref)
 
     for c in (r_e, r_i, r_w1, r_w2, r_dn):
         c.wait_send()
@@ -435,7 +464,19 @@
             d_give[i].wait_send()
     for x in (ag_n, rs_s, ag_s, rs_y, rs_d, ag_o):
         x.drain()
-    for c in (o_w2, o_w1, o_de, o_out):
+
+
+def rows_out(ids, o, de, dw1, dw2, out_ref, de_ref, dw1_ref, dw2_ref, buf, sem):
+    copies = [pltpu.make_async_copy(src, dst, sem.at[i]) for i, (src, dst) in enumerate(
+        ((dw1, dw1_ref), (dw2, dw2_ref), (de, de_ref), (buf, out_ref)))]
+    for c in copies[:3]:
+        c.start()
+    _, vocab, half = o.shape
+    mask = hot(ids[...], vocab)
+    buf[:half] = dot(o[0], mask, 0, 0).astype(BF)
+    buf[half:] = dot(o[1], mask, 0, 0)[:buf.shape[0] - half].astype(BF)
+    copies[3].start()
+    for c in copies:
         c.wait()
 
 
@@ -458,44 +499,53 @@
         vm = pltpu.VMEM
         dma = lambda *shape: pltpu.SemaphoreType.DMA(shape)
         scratch = dict(
-            es=vm((2, rows_e, width), BF), gsrc=vm((1, width), BF), ids=vm((2, 1, tokens), jnp.int32),
+            es=vm((2, rows_e, width), BF), gsrc=vm((width,), BF), ids=vm((2, 1, tokens), jnp.int32),
             w1s=vm((2, f_loc, width), BF), w2s=vm((2, f_loc, width), BF), dt=vm((2, half, tokens), BF),
             e24=vm((rb, 2 * half), F32), w1p=vm((2, f_chip, half), BF), w2p=vm((2, f_chip, half), BF),
             bn=vm((2, chips, 2 * rb, half // 2), BF), bo=vm((2, chips, 2 * rb, half // 2), BF),
             bs=vm((2, chips, rb, half), F32), sp=vm((6, vocab, half), BF),
-            n=vm((2, vocab, half), BF), o=vm((2, vocab, half), BF),
+            n=vm((2, vocab, half), BF),
             gs=vm((chips, rb, half), F32), gy=vm((chips, rb, half), F32), gd=vm((chips, rb, half), F32),
             lay=vm((3, 4, rb, half), F32), ra=vm((3, 2, 4, rb, half), F32), rb=vm((3, 3, rb, half), F32),
             r=vm((3, 4, rb, half), F32),
-            hid=vm((vocab, f_chip), BF), slope=vm((vocab, f_chip), F32),
-            dnx=vm((2, rb, half), F32), de=vm((rows_e, width), F32),
-            dw1=vm((f_loc, width), F32), dw2=vm((f_loc, width), F32), out=vm((width, tokens), BF),
-            lsem=dma(10), psem=dma(6), qsem=dma(6),
-            ss=dma(3, 15), sr=dma(3, 15),
+            hid=vm((vocab, f_chip), BF), slope=vm((chips, rb, f_chip), F32), dh=vm((chips, rb, f_chip), F32),
+            dnx=vm((2, rb, half), F32),
+            lsem=dma(6), psem=dma(6), qsem=dma(6),
+            gsem=dma(9), gd3=dma(3, 3), sr=dma(3, 15), gr=dma(3, 15),
         )
-        for name in 'nso':
-            scratch.update({name + 'ss': dma(15), name + 'rs': dma(15), name + 'ds': dma(chips), name + 'es': dma(chips)})
         names = list(scratch)
 
         def body(*refs):
             kernel(side, *refs[:10], dict(zip(names, refs[10:])))
 
-        hbm = pl.BlockSpec(memory_space=pl.ANY)
-        out_t, d_emb, dw1_t, d_w2 = pl.pallas_call(
+        hbm = pl.BlockSpec(memory_space=pltpu.HBM)
+        on_chip = pl.BlockSpec(memory_space=pltpu.VMEM)
+        shapes = (
+            jax.ShapeDtypeStruct((rows_e, width), F32),
+            jax.ShapeDtypeStruct((f_loc, width), F32),
+            jax.ShapeDtypeStruct((f_loc, width), F32),
+        )
+        ids_row = token_ids.reshape(1, tokens)
+        done = pl.pallas_call(
             body,
-            out_shape=(
-                jax.ShapeDtypeStruct((width, tokens), BF),
-                jax.ShapeDtypeStruct((rows_e, width), F32),
-                jax.ShapeDtypeStruct((f_loc, width), F32),
-                jax.ShapeDtypeStruct((f_loc, width), F32),
-            ),
+            out_shape=(jax.ShapeDtypeStruct((2, vocab, half), BF),) + shapes,
             in_specs=[hbm] * 6,
-            out_specs=(hbm,) * 4,
+            out_specs=(on_chip,) * 4,
             scratch_shapes=list(scratch.values()),
             compiler_params=pltpu.CompilerParams(
-                collective_id=0, has_side_effects=True, vmem_limit_bytes=60 * 1024 * 1024),
+                collective_id=0, has_side_effects=True, vmem_limit_bytes=36 * 1024 * 1024),
             name='step',
-        )(token_ids.reshape(1, tokens), emb_shard, norm_gain.reshape(1, width), w_up.T, w_down, grad_out.T)
+        )(*(pltpu.with_memory_space_constraint(v, pltpu.HBM) for v in (
+            ids_row, emb_shard, norm_gain, w_up.T, w_down, grad_out.T)))
+        out_t, d_emb, dw1_t, d_w2 = pl.pallas_call(
+            rows_out,
+            out_shape=(jax.ShapeDtypeStruct((width, tokens), BF),) + shapes,
+            in_specs=[on_chip] * 5,
+            out_specs=(hbm,) * 4,
+            scratch_shapes=[vm((width, tokens), BF), dma(4)],
+            compiler_params=pltpu.CompilerParams(vmem_limit_bytes=16 * 1024 * 1024),
+            name='rows_out',
+        )(ids_row, *done)
         return out_t.T, d_emb, dw1_t.T, d_w2
 
     return jax.shard_map(

time: 66.7 us -> 56.6 us (0.85)
  local copies, waits for them, and re-layouts: 6.23 us -> 0.01 us
  Pallas kernels: 59.6 us -> 55.9 us
    unnamed x12 -> x2, local copies, waits for them, and re-layouts: 5.63 us -> 0.01 us
    pallas_call x1 -> x2, Pallas kernels: 59.6 us -> 55.9 us  [the longest x1 54.4 us: local_step(): pl.pallas_call(body, out_shape=(jax.ShapeDtypeStruct((2, vocab, half), BF...]
where the time goes in v2:
time: 56.6 us; the launch traced here: 56.5 us
  Pallas kernels  55.9 us (99%)
  between operations  0.66 us (1%)
    pallas_call x1, Pallas kernels, local_step(): pl.pallas_call(body, out_shape=(jax.ShapeDtypeStruct((2, vocab, half), BF...  54.4 us
    pallas_call x1, Pallas kernels, local_step(): pl.pallas_call(rows_out, out_shape=(jax.ShapeDtypeStruct((width, tokens),...  1.5 us

profile of v2, /device:TPU:97, one launch (start us, length us, event | category | flops | bytes accessed | tf_op | source)
XLA Modules:
  0.0 56.5 jit_solution(3535596912138679903)
XLA Ops:
  0.6 0.0 copy-start
  0.6 54.4 %step.1 = (bf16[2,384,768]{2,1,0:T(8,128)(2,1)S(1)}, f32[12,1472]{1,0:T(8,128)S(1)}, f32[112,1472]{1,0:T(8,128)S(1)}, f32[112,1472]{1,0:T(8,128)S(1)}) custom-call(s32[1,256]{1,0:T(1,128)} %bitcast.5, bf16[12,1472]{1,0:T(8,128)(2,1)} %refs_1_.1, bf16[1472]{0:T(1024)(128)(2,1)} %refs_2_.1, bf16[112,1472]{1,0:T(8,128)(2,1)} %bitcast.8, ...), custom_call_target="tpu_custom_call" | custom-call | tf_op jit(solution)/shard_map/step/pallas_call | solution.py:529
  55.0 0.0 copy-done
  55.0 1.5 %rows_out.1 = (bf16[1472,256]{1,0:T(8,128)(2,1)}, f32[12,1472]{1,0:T(8,128)}, f32[112,1472]{1,0:T(8,128)}, f32[112,1472]{1,0:T(8,128)}) custom-call(s32[1,256]{1,0:T(1,128)S(1)} %bitcast.6, bf16[2,384,768]{2,1,0:T(8,128)(2,1)S(1)} %get-tuple-element.12.o, f32[12,1472]{1,0:T(8,128)S(1)} %get-tuple-element.13.de, f32[112,1472]{1,0:T(8,128)S(1)} %get-tuple-element.14.dw1, ...), custom_call_target="tpu_custom_call" | custom-call | tf_op jit(solution)/shard_map/rows_out/pallas_call | solution.py:540
Async XLA Ops:
  0.6 54.4 %copy-start = (s32[256]{0:T(256)S(1)}, s32[256]{0:T(256)}, u32[]{:S(2)}) copy-start(s32[256]{0:T(256)} %param.6) | copy-start | bytes 3076

commit v3 on v2

--- a/solution.py
+++ b/solution.py
@@ -82,47 +82,47 @@
     def c_ring(self, k, plus):
         da = 1 if plus else 3
         j = 0 if plus else 1
-        return self.copy(self.g.at[self.ring.at(da, k)], self.ra.at[j, k], 4 + 4 * j + k, self.ring.dev(da, 0))
+        return self.copy(self.g.at[self.ring.at(da, k)], self.ra.at[j, k], 4 + k, self.ring.dev(da, 0))
 
     def c_b(self, k):
-        return self.copy(self.r.at[k], self.rb.at[k - 1], 11 + k, self.ring.dev(0, k))
+        return self.copy(self.r.at[k], self.rb.at[k - 1], 8, self.ring.dev(0, k))
 
     def go(self, c):
         c.start()
         self.sent.append(c)
 
-    def start_relay(self):
-        for kp, km in zip(PLUS, MINUS):
+    def relays(self, j):
+        for kp, km in ((PLUS[j], MINUS[j]),):
             self.go(self.c_relay(kp))
             self.go(self.c_relay(km))
 
-    def start_own(self):
-        for kp, km in zip(MINUS, PLUS):
+    def owns(self, j):
+        for kp, km in ((MINUS[j], PLUS[j]),):
             self.go(self.c_ring(kp, True))
             self.go(self.c_ring(km, False))
 
-    def middle(self):
-        for kp, km in zip(PLUS, MINUS):
+    def middle(self, j):
+        for kp, km in ((PLUS[j], MINUS[j]),):
             for k, plus in ((kp, True), (km, False)):
                 self.c_relay(k).wait_recv()
                 blk = self.ring.at(1 if plus else 3, k)
                 self.g[blk] = self.g[blk] + self.relay[k]
                 self.go(self.c_ring(k, plus))
 
-    def short(self):
-        for k in (2, 3, 1, 0):
-            self.c_ring(k, True).wait_recv()
-            self.c_ring(k, False).wait_recv()
+    def short(self, *ks):
+        for k in ks:
+            self.arrived(2, 4 + k)
             self.r[k] = self.g[self.ring.at(0, k)] + self.ra[0, k] + self.ra[1, k]
             if k:
                 self.go(self.c_b(k))
 
     def finish(self):
-        acc = self.r[0]
-        for k in (1, 3, 2):
-            self.c_b(k).wait_recv()
-            acc = acc + self.rb[k - 1]
-        return acc
+        self.arrived(3, 8)
+        return self.r[0] + self.rb[0] + self.rb[2] + self.rb[1]
+
+    def arrived(self, blocks, i):
+        ref = self.g.at[pl.ds(0, blocks)]
+        pltpu.make_async_copy(ref, ref, self.rsem.at[i]).wait()
 
     def drain(self):
         whole = self.g.at[pl.ds(0, len(self.sent))]
@@ -133,8 +133,8 @@
 
 
 class Gather:
-    def __init__(self, ring, buf, ssem, rsem, dsem, esem):
-        self.ring, self.buf = ring, buf
+    def __init__(self, ring, buf, ssem, rsem, dsem, esem, direct=False):
+        self.ring, self.buf, self.direct = ring, buf, direct
         self.ssem, self.rsem, self.dsem, self.esem = ssem, rsem, dsem, esem
         self.sent = []
 
@@ -161,6 +161,8 @@
         blk = self.ring.at(0, self.back(k))
         self.go(self.copy(blk, k, self.ring.dev(1, 0)))
         self.go(self.copy(blk, 4 + k, self.ring.dev(3, 0)))
+        if self.direct:
+            self.go(self.copy(blk, 8 + k, self.ring.dev(2, 0)))
 
     def start(self):
         blk = self.ring.at(0, 0)
@@ -169,28 +171,28 @@
         self.both(0)
         self.over(blk, 0)
 
-    def first(self):
-        for k in (1, 3, 2):
+    def first(self, *ks):
+        for k in ks:
             blk = self.ring.at(0, self.back(k))
             self.copy(blk, 11 + k, self.ring.dev(0, k)).wait_recv()
             self.both(k)
             self.over(blk, 0)
 
-    def middle(self, ks=(0, 1, 3, 2)):
+    def middle(self, *ks):
         for k in ks:
             blk = self.ring.at(3, self.back(k))
             self.copy(blk, k, self.ring.dev(1, 0)).wait_recv()
-            if k in FWD_P:
+            if k in FWD_P and not self.direct:
                 self.go(self.copy(blk, 8 + k, self.ring.dev(1, 0)))
             self.over(blk, 1)
             blk = self.ring.at(1, self.back(k))
             self.copy(blk, 4 + k, self.ring.dev(3, 0)).wait_recv()
-            if k in FWD_M:
+            if k in FWD_M and not self.direct:
                 self.go(self.copy(blk, 8 + k, self.ring.dev(3, 0)))
             self.over(blk, 1)
 
-    def last(self):
-        for k in (0, 3, 1, 2):
+    def last(self, *ks):
+        for k in ks:
             blk = self.ring.at(2, self.back(k))
             self.copy(blk, 8 + k, self.ring.dev(1, 0)).wait_recv()
             self.over(blk, 2)
@@ -237,15 +239,22 @@
     c_w2 = local(w2_in, s['w2s'].at[core], 4)
     d_own = (local(d_in.at[:half], s['dt'].at[0], 5),
              local(d_in.at[half:], s['dt'].at[0, :rest], 5))
-    r_e = pair(e_in, s['es'].at[core], 0)
-    r_i = pair(ids_in, s['ids'].at[core], 1)
+    r_e = pair(s['es'].at[core], s['es'].at[core], 0)
+    r_i = pair(s['ids'].at[core], s['ids'].at[core], 1)
     r_w1 = pair(w1_in, s['w1s'].at[core], 2)
     r_w2 = pair(w2_in, s['w2s'].at[core], 3)
-    d_give = (pair(d_in.at[half:], s['dt'].at[1, :rest], 4),
-              pair(d_in.at[:half], s['dt'].at[1], 4))
-
-    for c in (c_e, c_g, c_i):
-        c.start()
+    d_load = (local(d_in.at[half:], s['dg'].at[:rest], 6),
+              local(d_in.at[:half], s['dg'], 6))
+    d_give = (pair(s['dg'].at[:rest], s['dt'].at[1, :rest], 4),
+              pair(s['dg'], s['dt'].at[1], 4))
+
+    c_e.start()
+    for i in range(2):
+        @pl.when(core == i)
+        def _():
+            d_load[i].start()
+    c_g.start()
+    c_i.start()
 
     @pl.when(core == 1)
     def _():
@@ -264,19 +273,21 @@
     c_w2.start()
     pl.semaphore_wait(barrier, len(peers))
 
+    c_e.wait()
     r_e.start()
-    r_i.start()
     for i in range(2):
         @pl.when(core == i)
         def _():
+            d_load[i].wait()
             d_give[i].start()
+    c_i.wait()
+    r_i.start()
     r_w1.start()
     r_w2.start()
 
     def wide(v):
         return jnp.concatenate([v, jnp.zeros((v.shape[0], 2 * half - width), F32)], axis=1)
 
-    c_e.wait()
     c_g.wait()
     r_e.wait_recv()
     gain = wide(s['gsrc'][...].astype(F32).reshape(1, width))
@@ -294,25 +305,68 @@
     s['bn'][core, chip] = pack(mine(x24 * inv_rms(x24) * gain))
     ag_n.start()
 
-    c_i.wait()
     for i in range(2):
         @pl.when(core == i)
         def _():
             d_own[i].wait()
-    tot = dot(hot(s['ids'][core], vocab), s['dt'][0], 1, 1)
+    def s_rows(da, src):
+        blks = [ring.at(da, k) for k in range(side)]
+        row = jnp.concatenate([rb * blk + lax.broadcasted_iota(jnp.int32, (rb, s['dt'].shape[2]), 0) for blk in blks], axis=0)
+        pick = jnp.where(row == s['ids'][core if src == 0 else 1 - core], 1.0, 0.0).astype(BF)
+        d = dot(pick, s['dt'][src], 1, 1)
+        for i, blk in enumerate(blks):
+            v = d[i * rb:(i + 1) * rb]
+            s['gs'][blk] = v if src == 0 else s['gs'][blk] + v
+
+    for da in range(side):
+        s_rows(da, 0)
     r_i.wait_recv()
     for i in range(2):
         @pl.when(core == i)
         def _():
             d_give[1 - i].wait_recv()
 
-    tot = tot + dot(hot(s['ids'][1 - core], vocab), s['dt'][1], 1, 1)
-    s['gs'][...] = tot.reshape(chips, rb, half)
+    s_rows(2, 1)
     rs_s = Scatter(ring, s['gs'], s['lay'].at[0], s['ra'].at[0], s['rb'].at[0], s['r'].at[0], s['gsem'].at[0], s['sr'].at[0])
-    rs_s.start_relay()
-    rs_s.start_own()
-
-    ag_n.first()
+    rs_s.relays(0)
+    rs_s.relays(1)
+    s_rows(1, 1)
+    s_rows(3, 1)
+    rs_s.owns(0)
+    rs_s.owns(1)
+    s_rows(0, 1)
+
+
+    def tall(v):
+        return jnp.concatenate(parts(v), axis=0)
+
+    def short(v):
+        n = v.shape[0] // 3
+        return v[2 * n:] + v[n:2 * n] + v[:n]
+
+    def dh_add(h, blks):
+        v = jnp.concatenate([s['bs'][h, blk] for blk in blks], axis=0)
+        d = short(dot(tall(v), s['w2p'][h], 1, 1))
+        for i, blk in enumerate(blks):
+            s['dh'][blk] = s['dh'][blk] + d[i * rb:(i + 1) * rb]
+
+    def line(da):
+        return [ring.at(da, k) for k in range(side)]
+
+    def cross(db):
+        return [ring.at(k, db) for k in range(side)]
+
+    def dn_rows(da):
+        blks = line(da)
+        du = [s['dh'][blk] * s['slope'][blk] for blk in blks]
+        for blk, v in zip(blks, du):
+            s['dh'][blk] = v
+        d = short(dot(tall(jnp.concatenate(du, axis=0)), s['w1p'][core], 1, 0))
+        for i, blk in enumerate(blks):
+            s['gd'][blk] = d[i * rb:(i + 1) * rb]
+
+    def own(v):
+        return jnp.where(core == 0, v[:, :f_loc], v[:, f_loc:])
 
     c_w1.wait()
     c_w2.wait()
@@ -325,10 +379,23 @@
             s[w_dst][1, rows, :] = jnp.concatenate(
                 [s[w_src][i, :, half:], jnp.zeros((f_loc, half - rest), BF)], axis=1)
 
-    rs_s.middle()
-    ag_n.middle()
-    rs_s.short()
-    ag_n.last()
+    ag_n.first(1)
+    ag_n.first(3)
+    ag_n.first(2)
+    rs_s.middle(0)
+    rs_s.middle(1)
+    ag_n.middle(0)
+    ag_n.middle(1)
+    ag_n.middle(3)
+    ag_n.middle(2)
+    rs_s.short(2)
+    rs_s.short(3)
+    rs_s.short(1)
+    rs_s.short(0)
+    ag_n.last(0)
+    ag_n.last(3)
+    ag_n.last(1)
+    ag_n.last(2)
     ag_n.finish()
 
     def unpack(buf, dst):
@@ -348,73 +415,55 @@
     s['dh'][...] = jnp.zeros((chips, rb, f_chip), F32)
     s['gy'][...] = dot(hid, s['w2p'][core], 1, 0).reshape(chips, rb, half)
 
-    rs_y = Scatter(ring, s['gy'], s['lay'].at[1], s['ra'].at[1], s['rb'].at[1], s['r'].at[1], s['gsem'].at[1], s['sr'].at[1])
     ag_s = Gather(ring, s['bs'], s['gsem'].at[4], s['gr'].at[1], s['gd3'].at[1], s['gsem'].at[7])
     s['bs'][core, chip] = rs_s.finish()
     ag_s.start()
     rs_y = Scatter(ring, s['gy'], s['lay'].at[1], s['ra'].at[1], s['rb'].at[1], s['r'].at[1], s['gsem'].at[1], s['sr'].at[1])
-    rs_y.start_relay()
-    rs_y.start_own()
-    ag_s.first()
-
-    def tall(v):
-        return jnp.concatenate(parts(v), axis=0)
-
-    def short(v):
-        n = v.shape[0] // 3
-        return v[2 * n:] + v[n:2 * n] + v[:n]
-
-    def dh_add(h, blks):
-        v = jnp.concatenate([s['bs'][h, blk] for blk in blks], axis=0)
-        d = short(dot(tall(v), s['w2p'][h], 1, 1))
-        for i, blk in enumerate(blks):
-            s['dh'][blk] = s['dh'][blk] + d[i * rb:(i + 1) * rb]
-
-    def line(da):
-        return [ring.at(da, k) for k in range(side)]
-
-    def cross(db):
-        return [ring.at(k, db) for k in range(side)]
-
-    def dn_rows(da):
-        blks = line(da)
-        du = [s['dh'][blk] * s['slope'][blk] for blk in blks]
-        for blk, v in zip(blks, du):
-            s['dh'][blk] = v
-        d = short(dot(tall(jnp.concatenate(du, axis=0)), s['w1p'][core], 1, 0))
-        for i, blk in enumerate(blks):
-            s['gd'][blk] = d[i * rb:(i + 1) * rb]
-
-    ag_s.middle((0,))
+    rs_y.relays(0)
+    rs_y.relays(1)
+    rs_y.owns(0)
+    rs_y.owns(1)
+    ag_s.first(1)
+    ag_s.first(3)
+    ag_s.first(2)
+    ag_s.middle(0)
     dh_add(core, line(0))
-    rs_y.middle()
-    ag_s.middle((1, 3, 2))
+    rs_y.middle(0)
+    rs_y.middle(1)
+    ag_s.middle(1)
+    ag_s.middle(3)
+    ag_s.middle(2)
     dh_add(core, line(1) + line(3))
     ag_s.passed(0)
     dh_add(1 - core, cross(0))
-    rs_y.short()
+    rs_y.short(2)
+    rs_y.short(3)
+    rs_y.short(1)
+    rs_y.short(0)
     ag_s.passed(1)
     dh_add(1 - core, cross(1) + cross(3))
-    ag_s.last()
+    ag_s.last(0)
+    ag_s.last(3)
+    ag_s.last(1)
+    ag_s.last(2)
     dh_add(core, line(2))
     ag_s.passed(2)
     dh_add(1 - core, cross(2))
-    rs_d = Scatter(ring, s['gd'], s['lay'].at[2], s['ra'].at[2], s['rb'].at[2], s['r'].at[2], s['gsem'].at[2], s['sr'].at[2])
+    rs_d = Scatter(ring, s['gd'], s['lay'].at[2], s['ra'].at[2], s['rb'].at[2], s['r'].at[2], s['gsem'].at[2], s['sr'].at[0])
     dn_rows(2)
-    rs_d.start_relay()
+    rs_d.relays(0)
+    rs_d.relays(1)
     dn_rows(1)
     dn_rows(3)
-    rs_d.start_own()
+    rs_d.owns(0)
+    rs_d.owns(1)
     dn_rows(0)
-    ag_o = Gather(ring, s['bo'], s['gsem'].at[5], s['gr'].at[2], s['gd3'].at[2], s['gsem'].at[8])
+    ag_o = Gather(ring, s['bo'], s['gsem'].at[5], s['gr'].at[0], s['gd3'].at[0], s['gsem'].at[8])
     s['bo'][core, chip] = pack(mine(s['e24'][...]) + rs_y.finish())
     ag_o.start()
     for i in range(2):
         for j, p in enumerate(parts(s['bs'][i].reshape(vocab, half))):
             s['sp'][3 * i + j] = p
-
-    def own(v):
-        return jnp.where(core == 0, v[:, :f_loc], v[:, f_loc:])
 
     hid_own = own(s['hid'][...].astype(F32)).astype(BF)
     for i in range(2):
@@ -426,9 +475,14 @@
         else:
             dw2_ref[:, half:] = acc[:, :rest]
 
-    rs_d.middle()
-    ag_o.first()
-
+    rs_d.middle(0)
+    rs_d.middle(1)
+    ag_o.first(1)
+    ag_o.first(3)
+    ag_o.first(2)
+    rs_d.short(2)
+    rs_d.short(3)
+    rs_d.short(1)
     du_own = parts(own(s['dh'][...].reshape(vocab, f_chip)))
     for i in range(2):
         acc = jnp.zeros((f_loc, half), F32)
@@ -439,12 +493,18 @@
         else:
             dw1_ref[:, half:] = acc[:, :rest]
 
-    rs_d.short()
-    ag_o.middle()
+    rs_d.short(0)
+    ag_o.middle(0)
+    ag_o.middle(1)
+    ag_o.middle(3)
+    ag_o.middle(2)
     s['dnx'][core] = rs_d.finish()
     r_dn = pair(s['dnx'].at[core], s['dnx'].at[core], 5)
     r_dn.start()
-    ag_o.last()
+    ag_o.last(0)
+    ag_o.last(3)
+    ag_o.last(1)
+    ag_o.last(2)
     pair(s['dnx'].at[1 - core], s['dnx'].at[1 - core], 5).wait_recv()
     inv = inv_rms(s['e24'][...])
     xr = s['e24'][...] * inv
@@ -456,6 +516,7 @@
     ag_o.finish()
     unpack(s['bo'], o_ref)
 
+
     for c in (r_e, r_i, r_w1, r_w2, r_dn):
         c.wait_send()
     for i in range(2):
@@ -467,15 +528,16 @@
 
 
 def rows_out(ids, o, de, dw1, dw2, out_ref, de_ref, dw1_ref, dw2_ref, buf, sem):
+    _, vocab, half = o.shape
     copies = [pltpu.make_async_copy(src, dst, sem.at[i]) for i, (src, dst) in enumerate(
-        ((dw1, dw1_ref), (dw2, dw2_ref), (de, de_ref), (buf, out_ref)))]
+        ((dw1, dw1_ref), (dw2, dw2_ref), (de, de_ref), (buf.at[:half], out_ref.at[:half]), (buf.at[half:], out_ref.at[half:])))]
     for c in copies[:3]:
         c.start()
-    _, vocab, half = o.shape
     mask = hot(ids[...], vocab)
     buf[:half] = dot(o[0], mask, 0, 0).astype(BF)
+    copies[3].start()
     buf[half:] = dot(o[1], mask, 0, 0)[:buf.shape[0] - half].astype(BF)
-    copies[3].start()
+    copies[4].start()
     for c in copies:
         c.wait()
 
@@ -500,7 +562,7 @@
         dma = lambda *shape: pltpu.SemaphoreType.DMA(shape)
         scratch = dict(
             es=vm((2, rows_e, width), BF), gsrc=vm((width,), BF), ids=vm((2, 1, tokens), jnp.int32),
-            w1s=vm((2, f_loc, width), BF), w2s=vm((2, f_loc, width), BF), dt=vm((2, half, tokens), BF),
+            w1s=vm((2, f_loc, width), BF), w2s=vm((2, f_loc, width), BF), dt=vm((2, half, tokens), BF), dg=vm((half, tokens), BF),
             e24=vm((rb, 2 * half), F32), w1p=vm((2, f_chip, half), BF), w2p=vm((2, f_chip, half), BF),
             bn=vm((2, chips, 2 * rb, half // 2), BF), bo=vm((2, chips, 2 * rb, half // 2), BF),
             bs=vm((2, chips, rb, half), F32), sp=vm((6, vocab, half), BF),
@@ -510,8 +572,8 @@
             r=vm((3, 4, rb, half), F32),
             hid=vm((vocab, f_chip), BF), slope=vm((chips, rb, f_chip), F32), dh=vm((chips, rb, f_chip), F32),
             dnx=vm((2, rb, half), F32),
-            lsem=dma(6), psem=dma(6), qsem=dma(6),
-            gsem=dma(9), gd3=dma(3, 3), sr=dma(3, 15), gr=dma(3, 15),
+            lsem=dma(7), psem=dma(6), qsem=dma(6),
+            gsem=dma(9), gd3=dma(2, 3), sr=dma(2, 9), gr=dma(2, 15),
         )
         names = list(scratch)
 
@@ -542,7 +604,7 @@
             out_shape=(jax.ShapeDtypeStruct((width, tokens), BF),) + shapes,
             in_specs=[on_chip] * 5,
             out_specs=(hbm,) * 4,
-            scratch_shapes=[vm((width, tokens), BF), dma(4)],
+            scratch_shapes=[vm((width, tokens), BF), dma(5)],
             compiler_params=pltpu.CompilerParams(vmem_limit_bytes=16 * 1024 * 1024),
             name='rows_out',
         )(ids_row, *done)

time: 56.6 us -> 56.1 us (level)
  Pallas kernels: 55.9 us -> 55.3 us
where the time goes in v3:
time: 56.1 us; the launch traced here: 56 us
  Pallas kernels  55.3 us (99%)
  between operations  0.66 us (1%)
    pallas_call x1, Pallas kernels, local_step(): pl.pallas_call(body, out_shape=(jax.ShapeDtypeStruct((2, vocab, half), BF...  53.8 us
    pallas_call x1, Pallas kernels, local_step(): pl.pallas_call(rows_out, out_shape=(jax.ShapeDtypeStruct((width, tokens),...  1.5 us

profile of v3, /device:TPU:97, one launch (start us, length us, event | category | flops | bytes accessed | tf_op | source)
XLA Modules:
  0.0 56.0 jit_solution(13286953442961944354)
XLA Ops:
  0.6 0.0 copy-start
  0.6 53.8 %step.1 = (bf16[2,384,768]{2,1,0:T(8,128)(2,1)S(1)}, f32[12,1472]{1,0:T(8,128)S(1)}, f32[112,1472]{1,0:T(8,128)S(1)}, f32[112,1472]{1,0:T(8,128)S(1)}) custom-call(s32[1,256]{1,0:T(1,128)} %bitcast.5, bf16[12,1472]{1,0:T(8,128)(2,1)} %refs_1_.1, bf16[1472]{0:T(1024)(128)(2,1)} %refs_2_.1, bf16[112,1472]{1,0:T(8,128)(2,1)} %bitcast.8, ...), custom_call_target="tpu_custom_call" | custom-call | tf_op jit(solution)/shard_map/step/pallas_call | solution.py:591
  54.5 0.0 copy-done
  54.5 1.5 %rows_out.1 = (bf16[1472,256]{1,0:T(8,128)(2,1)}, f32[12,1472]{1,0:T(8,128)}, f32[112,1472]{1,0:T(8,128)}, f32[112,1472]{1,0:T(8,128)}) custom-call(s32[1,256]{1,0:T(1,128)S(1)} %bitcast.6, bf16[2,384,768]{2,1,0:T(8,128)(2,1)S(1)} %get-tuple-element.12.o, f32[12,1472]{1,0:T(8,128)S(1)} %get-tuple-element.13.de, f32[112,1472]{1,0:T(8,128)S(1)} %get-tuple-element.14.dw1, ...), custom_call_target="tpu_custom_call" | custom-call | tf_op jit(solution)/shard_map/rows_out/pallas_call | solution.py:602
Async XLA Ops:
  0.6 53.8 %copy-start = (s32[256]{0:T(256)S(1)}, s32[256]{0:T(256)}, u32[]{:S(2)}) copy-start(s32[256]{0:T(256)} %param.6) | copy-start | bytes 3076

commit v4 on v3

--- a/solution.py
+++ b/solution.py
@@ -61,7 +61,7 @@
         return {'tensor': self.at(da, db) * CORES + self.core}
 
 
-PLUS, MINUS = (2, 1), (3, 0)
+PLUS, MINUS = (2, 3), (1, 0)
 
 
 class Scatter:
@@ -318,8 +318,7 @@
             v = d[i * rb:(i + 1) * rb]
             s['gs'][blk] = v if src == 0 else s['gs'][blk] + v
 
-    for da in range(side):
-        s_rows(da, 0)
+    s_rows(2, 0)
     r_i.wait_recv()
     for i in range(2):
         @pl.when(core == i)
@@ -330,11 +329,13 @@
     rs_s = Scatter(ring, s['gs'], s['lay'].at[0], s['ra'].at[0], s['rb'].at[0], s['r'].at[0], s['gsem'].at[0], s['sr'].at[0])
     rs_s.relays(0)
     rs_s.relays(1)
-    s_rows(1, 1)
-    s_rows(3, 1)
+    for da in (1, 3):
+        for src in range(2):
+            s_rows(da, src)
     rs_s.owns(0)
     rs_s.owns(1)
-    s_rows(0, 1)
+    for src in range(2):
+        s_rows(0, src)
 
 
     def tall(v):
@@ -437,8 +438,8 @@
     ag_s.passed(0)
     dh_add(1 - core, cross(0))
     rs_y.short(2)
+    rs_y.short(1)
     rs_y.short(3)
-    rs_y.short(1)
     rs_y.short(0)
     ag_s.passed(1)
     dh_add(1 - core, cross(1) + cross(3))
@@ -480,9 +481,10 @@
     ag_o.first(1)
     ag_o.first(3)
     ag_o.first(2)
+    ag_o.middle(0)
     rs_d.short(2)
+    rs_d.short(1)
     rs_d.short(3)
-    rs_d.short(1)
     du_own = parts(own(s['dh'][...].reshape(vocab, f_chip)))
     for i in range(2):
         acc = jnp.zeros((f_loc, half), F32)
@@ -494,7 +496,6 @@
             dw1_ref[:, half:] = acc[:, :rest]
 
     rs_d.short(0)
-    ag_o.middle(0)
     ag_o.middle(1)
     ag_o.middle(3)
     ag_o.middle(2)

time: 56.1 us -> 55.5 us (0.989)
  Pallas kernels: 55.3 us -> 54.7 us
    pallas_call x1, Pallas kernels: 53.8 us -> 53.2 us  [local_step(): pl.pallas_call(body, out_shape=(jax.ShapeDtypeStruct((2, vocab, half), BF...]
where the time goes in v4:
time: 55.5 us; the launch traced here: 55.4 us
  Pallas kernels  54.7 us (99%)
  between operations  0.66 us (1%)
    pallas_call x1, Pallas kernels, local_step(): pl.pallas_call(body, out_shape=(jax.ShapeDtypeStruct((2, vocab, half), BF...  53.2 us
    pallas_call x1, Pallas kernels, local_step(): pl.pallas_call(rows_out, out_shape=(jax.ShapeDtypeStruct((width, tokens),...  1.51 us

profile of v4, /device:TPU:97, one launch (start us, length us, event | category | flops | bytes accessed | tf_op | source)
XLA Modules:
  0.0 55.4 jit_solution(10856367047023522422)
XLA Ops:
  0.6 0.0 copy-start
  0.6 53.2 %step.1 = (bf16[2,384,768]{2,1,0:T(8,128)(2,1)S(1)}, f32[12,1472]{1,0:T(8,128)S(1)}, f32[112,1472]{1,0:T(8,128)S(1)}, f32[112,1472]{1,0:T(8,128)S(1)}) custom-call(s32[1,256]{1,0:T(1,128)} %bitcast.5, bf16[12,1472]{1,0:T(8,128)(2,1)} %refs_1_.1, bf16[1472]{0:T(1024)(128)(2,1)} %refs_2_.1, bf16[112,1472]{1,0:T(8,128)(2,1)} %bitcast.8, ...), custom_call_target="tpu_custom_call" | custom-call | tf_op jit(solution)/shard_map/step/pallas_call | solution.py:592
  53.9 0.0 copy-done
  53.9 1.5 %rows_out.1 = (bf16[1472,256]{1,0:T(8,128)(2,1)}, f32[12,1472]{1,0:T(8,128)}, f32[112,1472]{1,0:T(8,128)}, f32[112,1472]{1,0:T(8,128)}) custom-call(s32[1,256]{1,0:T(1,128)S(1)} %bitcast.6, bf16[2,384,768]{2,1,0:T(8,128)(2,1)S(1)} %get-tuple-element.12.o, f32[12,1472]{1,0:T(8,128)S(1)} %get-tuple-element.13.de, f32[112,1472]{1,0:T(8,128)S(1)} %get-tuple-element.14.dw1, ...), custom_call_target="tpu_custom_call" | custom-call | tf_op jit(solution)/shard_map/rows_out/pallas_call | solution.py:603
Async XLA Ops:
  0.6 53.2 %copy-start = (s32[256]{0:T(256)S(1)}, s32[256]{0:T(256)}, u32[]{:S(2)}) copy-start(s32[256]{0:T(256)} %param.6) | copy-start | bytes 3076

commit v5 on v4

--- a/solution.py
+++ b/solution.py
@@ -428,8 +428,8 @@
     ag_s.first(3)
     ag_s.first(2)
     ag_s.middle(0)
+    rs_y.middle(0)
     dh_add(core, line(0))
-    rs_y.middle(0)
     rs_y.middle(1)
     ag_s.middle(1)
     ag_s.middle(3)

time: 55.5 us -> 55.5 us (level)
  no operation moved by 1% of the time
where the time goes in v5:
time: 55.5 us; the launch traced here: 55.4 us
  Pallas kernels  54.7 us (99%)
  between operations  0.66 us (1%)
    pallas_call x1, Pallas kernels, local_step(): pl.pallas_call(body, out_shape=(jax.ShapeDtypeStruct((2, vocab, half), BF...  53.2 us
    pallas_call x1, Pallas kernels, local_step(): pl.pallas_call(rows_out, out_shape=(jax.ShapeDtypeStruct((width, tokens),...  1.51 us

profile of v5, /device:TPU:97, one launch (start us, length us, event | category | flops | bytes accessed | tf_op | source)
XLA Modules:
  0.0 55.4 jit_solution(12833780674918944198)
XLA Ops:
  0.6 0.0 copy-start
  0.6 53.2 %step.1 = (bf16[2,384,768]{2,1,0:T(8,128)(2,1)S(1)}, f32[12,1472]{1,0:T(8,128)S(1)}, f32[112,1472]{1,0:T(8,128)S(1)}, f32[112,1472]{1,0:T(8,128)S(1)}) custom-call(s32[1,256]{1,0:T(1,128)} %bitcast.5, bf16[12,1472]{1,0:T(8,128)(2,1)} %refs_1_.1, bf16[1472]{0:T(1024)(128)(2,1)} %refs_2_.1, bf16[112,1472]{1,0:T(8,128)(2,1)} %bitcast.8, ...), custom_call_target="tpu_custom_call" | custom-call | tf_op jit(solution)/shard_map/step/pallas_call | solution.py:592
  53.9 0.0 copy-done
  53.9 1.5 %rows_out.1 = (bf16[1472,256]{1,0:T(8,128)(2,1)}, f32[12,1472]{1,0:T(8,128)}, f32[112,1472]{1,0:T(8,128)}, f32[112,1472]{1,0:T(8,128)}) custom-call(s32[1,256]{1,0:T(1,128)S(1)} %bitcast.6, bf16[2,384,768]{2,1,0:T(8,128)(2,1)S(1)} %get-tuple-element.12.o, f32[12,1472]{1,0:T(8,128)S(1)} %get-tuple-element.13.de, f32[112,1472]{1,0:T(8,128)S(1)} %get-tuple-element.14.dw1, ...), custom_call_target="tpu_custom_call" | custom-call | tf_op jit(solution)/shard_map/rows_out/pallas_call | solution.py:603
Async XLA Ops:
  0.6 53.2 %copy-start = (s32[256]{0:T(256)S(1)}, s32[256]{0:T(256)}, u32[]{:S(2)}) copy-start(s32[256]{0:T(256)} %param.6) | copy-start | bytes 3076
